TPU v7x, 128 devices: a whole 4x4x4 slice. The times are simulated.
128 devices in a mesh: kpt: 1, col: 64 (over z, y, x), row: 2 (over core).
Axes of the slice: x: 4, y: 4, z: 4, core: 2. Of those that a mesh axis runs over, the one named last changes fastest.
Arguments:
- z_in: float32 [6144, 4096], P('kpt', ('col', 'row'))
- v_panels: float32 [6144, 6144], P(('kpt', 'row'), 'col')
- t_factors: float32 [192, 32, 32], P('kpt')
Outputs:
- output: float32 [6144, 4096], P(('kpt', 'row'), 'col')
All inputs are finite; a program needn't handle non-finite values.
Results may differ from a plain program's by a relative error of at most 0.001.
Values sent between devices are 32-bit elements.
A program may use at most 1 GiB of HBM per device.

v0:
```python
import jax
import jax.numpy as jnp
from jax import lax
from jax.sharding import PartitionSpec as P

PRECISE = lax.Precision.HIGHEST


def solution(mesh):
    col_count = mesh.shape["col"]

    def local_run(z_cols, v_local, t_local):
        panel_width = t_local.shape[-1]
        group_count = v_local.shape[1] // panel_width
        z_cur = lax.all_to_all(z_cols, "row", 0, 1, tiled=True)

        def group_step(step_idx, z_acc):
            group_idx = group_count - 1 - step_idx
            own_panel = lax.dynamic_slice_in_dim(v_local, group_idx * panel_width, panel_width, axis=1)
            gathered = lax.all_gather(own_panel, "col")

            def panel_step(inner_idx, z_val):
                owner_col = col_count - 1 - inner_idx
                panel = lax.dynamic_index_in_dim(gathered, owner_col, axis=0, keepdims=False)
                t_mat = lax.dynamic_index_in_dim(t_local, group_idx * col_count + owner_col, axis=0, keepdims=False)
                s_part = jnp.einsum("lb,lm->bm", panel, z_val, precision=PRECISE, preferred_element_type=jnp.float32)
                s_full = lax.psum(s_part, "row")
                w_full = jnp.dot(t_mat, s_full, precision=PRECISE, preferred_element_type=jnp.float32)
                return z_val - jnp.dot(panel, w_full, precision=PRECISE, preferred_element_type=jnp.float32)

            return lax.fori_loop(0, col_count, panel_step, z_acc)

        return lax.fori_loop(0, group_count, group_step, z_cur)

    return jax.shard_map(
        local_run,
        mesh=mesh,
        in_specs=(P("kpt", ("col", "row")), P(("kpt", "row"), "col"), P("kpt", None, None)),
        out_specs=P(("kpt", "row"), "col"),
        check_vma=False,
    )
```

profile of v0, /device:TPU:1, one launch (start us, length us, event | category | flops | bytes accessed | tf_op | source)
XLA Modules:
  0.0 3479.0 jit_solution(11111932464587329995)
XLA Ops:
  8.7 4.9 all-to-all-start
  16.4 3455.2 %while.44 = (s32[]{:T(128)}, f32[3072,64]{0,1:T(8,128)S(1)}, f32[3072,96]{0,1:T(8,128)}, f32[192,32,32]{2,1,0:T(8,128)}, s32[]{:T(128)}, /*index=5*/s32[]{:T(128...) while((s32[]{:T(128)}, f32[3072,64]{0,1:T(8,128)S(1)}, ...), condition=%wide.region_4.5_spmd, body=%wide.region_0.4_spmd.sunk | while | flops 151980032 | bytes 160498224 | solution.py:33
  19.1 396.1 %all-gather.5.cloned.1.call-done = f32[196608,32]{1,0:T(8,128)} async-done(((f32[3072,32]{1,0:T(8,128)}), f32[196608,32]{1,0:T(8,128)}) %all-gather.5.cloned.1.call-update) | async-done | bytes 25165840 | tf_op jit(solution)/shard_map/while/body/eval_jaxpr/all_gather | solution.py:20
  415.1 754.8 %while.45 = (s32[]{:T(128)}, f32[3072,64]{0,1:T(8,128)S(1)}, f32[64,3072,32]{2,1,0:T(8,128)}, s32[]{:T(128)}, f32[192,32,32]{2,1,0:T(8,128)}, /*index=5*/s32[]{:T(128)}, s32[]{:T(128)}, s32[]{:T(128)}, s32[]{:T(128)}, s32[]{:T(128)}) while((s32[]{:T(128)}, f32[3072,64]{0,1:T(8,128)S(1)}, f32[64,3072,32]{2,1,0:T(8,128)}, s32[]{:T(128)}, ...), condition=%wide.region_3.3_spmd, body=%wide.region_1.2_spmd.sunk | while | flops 151980032 | bytes 5570773 | solution.py:31
  419.1 4.1 psum.14
  427.6 4.0 fusion.28
  439.3 4.0 fusion.28
  451.2 4.0 fusion.28
  462.9 4.0 fusion.28
  474.7 4.0 fusion.28
  486.4 4.0 fusion.28
  521.9 4.0 fusion.28
  545.4 4.0 fusion.28
  557.1 4.0 fusion.28
  616.1 4.0 fusion.28
  627.8 4.0 fusion.28
  686.9 4.0 fusion.28
  698.6 4.0 fusion.28
  722.1 4.0 fusion.28
  757.6 4.0 fusion.28
  769.3 4.0 fusion.28
  781.1 4.0 fusion.28
  792.8 4.0 fusion.28
  828.3 4.0 fusion.28
  840.0 4.0 fusion.28
  851.9 4.0 fusion.28
  863.6 4.0 fusion.28
  899.0 4.0 fusion.28
  910.7 4.0 fusion.28
  922.6 4.0 fusion.28
  934.3 4.0 fusion.28
  969.7 4.0 fusion.28
  993.3 4.0 fusion.28
  1005.0 4.0 fusion.28
  1064.0 4.0 fusion.28
  1075.7 4.0 fusion.28
  1134.7 4.0 fusion.28
  1146.4 4.0 fusion.28
  1172.7 393.3 %all-gather.5.cloned.1.call-done = f32[196608,32]{1,0:T(8,128)} async-done(((f32[3072,32]{1,0:T(8,128)}), f32[196608,32]{1,0:T(8,128)}) %all-gather.5.cloned.1.call-update) | async-done | bytes 25165840 | tf_op jit(solution)/shard_map/while/body/eval_jaxpr/all_gather | solution.py:20
  1566.0 754.8 %while.45 = (s32[]{:T(128)}, f32[3072,64]{0,1:T(8,128)S(1)}, f32[64,3072,32]{2,1,0:T(8,128)}, s32[]{:T(128)}, f32[192,32,32]{2,1,0:T(8,128)}, /*index=5*/s32[]{:T(128)}, s32[]{:T(128)}, s32[]{:T(128)}, s32[]{:T(128)}, s32[]{:T(128)}) while((s32[]{:T(128)}, f32[3072,64]{0,1:T(8,128)S(1)}, f32[64,3072,32]{2,1,0:T(8,128)}, s32[]{:T(128)}, ...), condition=%wide.region_3.3_spmd, body=%wide.region_1.2_spmd.sunk | while | flops 151980032 | bytes 5570773 | solution.py:31
  1570.0 4.1 psum.14
  1578.4 4.0 fusion.28
  1625.6 4.0 fusion.28
  1637.3 4.0 fusion.28
  1649.1 4.0 fusion.28
  1696.3 4.0 fusion.28
  1708.0 4.0 fusion.28
  1719.8 4.0 fusion.28
  1731.5 4.0 fusion.28
  1767.0 4.0 fusion.28
  1778.7 4.0 fusion.28
  1790.6 4.0 fusion.28
  1802.3 4.0 fusion.28
  1849.4 4.0 fusion.28
  1861.3 4.0 fusion.28
  1873.0 4.0 fusion.28
  1920.1 4.0 fusion.28
  1932.0 4.0 fusion.28
  1943.7 4.0 fusion.28
  2002.7 4.0 fusion.28
  2014.4 4.0 fusion.28
  2323.6 393.3 %all-gather.5.cloned.1.call-done = f32[196608,32]{1,0:T(8,128)} async-done(((f32[3072,32]{1,0:T(8,128)}), f32[196608,32]{1,0:T(8,128)}) %all-gather.5.cloned.1.call-update) | async-done | bytes 25165840 | tf_op jit(solution)/shard_map/while/body/eval_jaxpr/all_gather | solution.py:20
  2716.8 754.8 %while.45 = (s32[]{:T(128)}, f32[3072,64]{0,1:T(8,128)S(1)}, f32[64,3072,32]{2,1,0:T(8,128)}, s32[]{:T(128)}, f32[192,32,32]{2,1,0:T(8,128)}, /*index=5*/s32[]{:T(128)}, s32[]{:T(128)}, s32[]{:T(128)}, s32[]{:T(128)}, s32[]{:T(128)}) while((s32[]{:T(128)}, f32[3072,64]{0,1:T(8,128)S(1)}, f32[64,3072,32]{2,1,0:T(8,128)}, s32[]{:T(128)}, ...), condition=%wide.region_3.3_spmd, body=%wide.region_1.2_spmd.sunk | while | flops 151980032 | bytes 5570773 | solution.py:31
  2720.8 4.1 psum.14
  (730 shorter events, 2047.4 us)
Async XLA Ops:
  6.5 7.0 copy-start
  8.7 7.7 all-to-all-start
  16.4 398.8 %all-gather.5.cloned.1.call-start = ((), (), s32[]{:S(2)}) async-start(), calls=%async_computation.1 | async-start | bytes 102236160 | tf_op jit(solution)/shard_map/while/body/eval_jaxpr/all_gather | solution.py:20
  1170.0 396.0 %all-gather.5.cloned.1.call-start = ((), (), s32[]{:S(2)}) async-start(), calls=%async_computation.1 | async-start | bytes 102236160 | tf_op jit(solution)/shard_map/while/body/eval_jaxpr/all_gather | solution.py:20
  2320.8 396.0 %all-gather.5.cloned.1.call-start = ((), (), s32[]{:S(2)}) async-start(), calls=%async_computation.1 | async-start | bytes 102236160 | tf_op jit(solution)/shard_map/while/body/eval_jaxpr/all_gather | solution.py:20
Sparse Core Ops, SparseCore 0:
  19.9 395.1 all-gather.4
  1173.5 392.3 all-gather.4
  2324.4 392.3 all-gather.4
where the time goes:
time: 3500 us; the launch traced here: 3480 us
  matrix products  1590 us (45%)
  waiting for transfers between devices  1180 us (34%)
  blocking collectives  663 us (19%)
    all_gather x3, waiting for transfers between devices, group_step(): gathered = lax.all_gather(own_panel, 'col')  1180 us
    dot_general x192, matrix products, panel_step(): jnp.einsum('lb,lm->bm', panel, z_val, precision=PRECISE, preferred_elemen...  765 us
    dot_general x192, matrix products, panel_step(): jnp.dot(panel, w_full, precision=PRECISE, preferred_element_type=jnp.floa...  666 us
    psum x192, blocking collectives, panel_step(): s_full = lax.psum(s_part, 'row')  663 us
    dot_general x192, matrix products, panel_step(): jnp.dot(t_mat, s_full, precision=PRECISE, preferred_element_type=jnp.floa...  162 us
  transfers between devices with their start and end apart: 4, of which 3 were waited for; matrix products, arithmetic and copies ran while one was open for 0% of the time, Pallas kernels for 0%

commit v1 on v0

v1 whole, which is shorter than its diff:
```python
import jax
import jax.numpy as jnp
from jax import lax
from jax.experimental import pallas as pl
from jax.experimental.pallas import tpu as pltpu
from jax.sharding import PartitionSpec as P

PRECISE = lax.Precision.HIGHEST
MESH = pl.DeviceIdType.MESH

SIDE = 4
BLK = 32
ROUNDS = 3
LANES = 128
CHUNKS = 24
GROUP = 256
STEPS = 24
COLS = 64

ORDER = (("x", "y", "z"), ("y", "z", "x"), ("z", "x", "y"))
SHARES = {
    24: (8, 8, 8), 22: (8, 7, 7), 20: (7, 7, 6), 18: (6, 6, 6),
    16: (5, 5, 6), 14: (5, 5, 4), 12: (4, 4, 4), 10: (3, 3, 4),
    8: (3, 3, 2), 6: (2, 2, 2), 4: (1, 1, 2), 2: (1, 1, 0),
}
ROUND_BASE = (0, 24, 40)
SLOTS = 48
KINDS = ("A+", "A-", "F+", "F-")


def part(rnd, z_src, colour):
    first = 8 * rnd + 2 * z_src
    shares = SHARES[CHUNKS - first]
    return ROUND_BASE[rnd] + first - 8 * rnd + sum(shares[:colour]), shares[colour]


def sem_table():
    table = {}
    for rnd in range(ROUNDS):
        for colour in range(3):
            for phase in range(3):
                planes = range(SIDE) if "z" in ORDER[colour][:phase] else (None,)
                for kind in KINDS:
                    for plane in planes:
                        table[rnd, colour, phase, kind, plane] = len(table)
    return table


SEMS = sem_table()


class Gather:
    def __init__(self, buf, send_sems, recv_sems):
        col = lax.axis_index("col")
        self.kpt, self.core = lax.axis_index("kpt"), lax.axis_index("row")
        self.me = {"z": col // 16, "y": (col // 4) % 4, "x": col % 4}
        self.buf, self.send_sems, self.recv_sems = buf, send_sems, recv_sems
        self.at = {(axis, offset): (self.me[axis] + offset) % SIDE for axis in "xyz" for offset in (1, 2, 3)}
        self.peer = {(axis, offset): self.find(axis, offset) for axis in "xyz" for offset in (1, 3)}

    def find(self, axis, offset):
        at = dict(self.me)
        at[axis] = self.at[axis, offset]
        return (self.kpt, at["z"] * 16 + at["y"] * 4 + at["x"], self.core)

    def shifted(self, axis, offset):
        return self.me[axis] if offset == 0 else self.at[axis, offset % SIDE]

    def neighbour(self, axis, offset):
        return self.peer[axis, offset % SIDE]

    def each(self, rnd, colour, phase, kind, source, fn):
        axis = ORDER[colour][phase]
        whole = ORDER[colour][:phase]
        rows = {"A+": pl.ds(0, BLK), "A-": pl.ds(0, BLK), "F+": pl.ds(0, BLK // 2), "F-": pl.ds(BLK // 2, BLK // 2)}[kind]
        target = self.neighbour(axis, 1 if kind[1] == "+" else -1)

        def descriptor(plane, sem):
            slot, count = part(rnd, plane, colour)
            if count == 0:
                return
            at = {}
            for name in "zyx":
                if name in whole:
                    at[name] = slice(None)
                else:
                    at[name] = self.shifted(name, source) if name == axis else self.me[name]
            block = self.buf.at[pl.ds(slot, count), plane, at["y"], at["x"], rows, :]
            fn(
                pltpu.make_async_remote_copy(
                    src_ref=block, dst_ref=block,
                    send_sem=self.send_sems.at[sem], recv_sem=self.recv_sems.at[sem],
                    device_id=target, device_id_type=MESH,
                )
            )

        if "z" in whole:
            for plane in reversed(range(SIDE)):
                descriptor(plane, SEMS[rnd, colour, phase, kind, plane])
            return
        plane_here = self.shifted("z", source) if axis == "z" else self.me["z"]
        for plane in range(SIDE):
            pl.when(plane_here == plane)(
                lambda plane=plane: descriptor(plane, SEMS[rnd, colour, phase, kind, None])
            )

    def start_own(self, rnd, colour, phase):
        for kind in ("A+", "A-"):
            self.each(rnd, colour, phase, kind, 0, lambda copy: copy.start())

    def forward(self, rnd, colour, phase):
        for kind, relay, source in (("A+", "F+", -1), ("A-", "F-", 1)):
            self.each(rnd, colour, phase, kind, source, lambda copy: copy.wait_recv())
            self.each(rnd, colour, phase, relay, source, lambda copy: copy.start())

    def finish(self, rnd, colour, phase):
        for kind, source in (("F+", -2), ("F-", 2)):
            self.each(rnd, colour, phase, kind, source, lambda copy: copy.wait_recv())

    def event(self, name, rnd):
        for colour in range(3):
            if name == "A1":
                self.start_own(rnd, colour, 0)
            elif name in ("F1", "F2", "F3"):
                self.forward(rnd, colour, int(name[1]) - 1)
            elif name in ("A2", "A3"):
                self.finish(rnd, colour, int(name[1]) - 2)
                self.start_own(rnd, colour, int(name[1]) - 1)
            else:
                self.finish(rnd, colour, 2)

    def drain(self):
        for rnd in range(ROUNDS):
            for colour in range(3):
                for phase in range(3):
                    for kind, source in (("A+", 0), ("A-", 0), ("F+", -1), ("F-", 1)):
                        self.each(rnd, colour, phase, kind, source, lambda copy: copy.wait_send())


EVENTS = (
    ("A1", 2), ("A1", 1), ("A1", 0), ("F1", 2), ("A2", 2), ("F1", 1), ("F2", 2), ("A3", 2),
    ("A2", 1), ("F1", 0), ("F3", 2), ("F2", 1), ("A2", 0), ("A3", 1), ("F2", 0), ("F3", 1),
    ("A3", 0), ("D", 2), ("D", 1), ("F3", 0), ("D", 0),
)


def nt(lhs, rhs):
    return lax.dot_general(lhs, rhs, (((1,), (1,)), ((), ())), precision=PRECISE, preferred_element_type=jnp.float32)


def nn(lhs, rhs):
    return lax.dot_general(lhs, rhs, (((1,), (0,)), ((), ())), precision=PRECISE, preferred_element_type=jnp.float32)


def enter(gather, partner):
    barrier = pltpu.get_barrier_semaphore()
    peers = [] if gather is None else [gather.neighbour(axis, offset) for axis in "xyz" for offset in (1, -1)]
    for peer in peers + ([] if partner is None else [partner]):
        pl.semaphore_signal(barrier, inc=1, device_id=peer, device_id_type=MESH)
    pl.semaphore_wait(barrier, len(peers) + (partner is not None))


def gather_kernel(v_ref, out_ref, buf, send_sems, recv_sems, own_sems):
    gather = Gather(buf, send_sems, recv_sems)
    me = gather.me
    own = []
    for rnd in range(ROUNDS):
        copy = pltpu.make_async_copy(
            v_ref.at[rnd, pl.ds(8 * rnd, CHUNKS - 8 * rnd)],
            buf.at[pl.ds(ROUND_BASE[rnd], CHUNKS - 8 * rnd), me["z"], me["y"], me["x"]],
            own_sems.at[rnd],
        )
        copy.start()
        own.append(copy)
    enter(gather, None)
    for copy in own:
        copy.wait()
    for name, rnd in EVENTS:
        gather.event(name, rnd)
    gather.drain()
    whole = pltpu.make_async_copy(buf, out_ref, own_sems.at[0])
    whole.start()
    whole.wait()


def apply_kernel(z_ref, v_ref, t_ref, out_ref, buf, acc, peer, t_buf, v_sems, peer_send, peer_recv, t_sems):
    partner = (lax.axis_index("kpt"), lax.axis_index("col"), 1 - lax.axis_index("row"))

    def v_copy(rnd):
        block = pl.ds(ROUND_BASE[rnd], CHUNKS - 8 * rnd)
        return pltpu.make_async_copy(v_ref.at[block], buf.at[block], v_sems.at[rnd])

    for rnd in reversed(range(ROUNDS)):
        v_copy(rnd).start()
    enter(None, partner)
    out_ref[...] = z_ref[...]

    row = lax.broadcasted_iota(jnp.int32, (GROUP, GROUP), 0)
    column = lax.broadcasted_iota(jnp.int32, (GROUP, GROUP), 1)

    def t_copy(group, slot):
        return pltpu.make_async_copy(t_ref.at[group], t_buf.at[slot], t_sems.at[slot])

    t_copy(STEPS - 1, 0).start()

    def step(idx, _):
        for rnd_needed in range(ROUNDS):
            pl.when(idx == 16 - 8 * rnd_needed)(lambda rnd_needed=rnd_needed: v_copy(rnd_needed).wait())

        group = STEPS - 1 - idx
        rnd = group // 8
        plane = (group % 8) // 2
        pair = (group % 2) * 2
        slot = idx % 2
        shift = 16 * rnd - 4 * rnd * (rnd - 1)
        first = 4 * rnd + plane

        def tile(w):
            halves = [
                buf[shift + 2 * w + half, plane, pl.ds(pair, 2), :, :, :].reshape(GROUP, LANES) for half in range(2)
            ]
            return jnp.concatenate(halves, axis=1)

        def z_tile(w):
            return jnp.concatenate([out_ref[2 * w], out_ref[2 * w + 1]], axis=1)

        acc[...] = jnp.zeros_like(acc)

        def gram(w, _):
            v = tile(w)
            acc[...] += nt(jnp.concatenate([z_tile(w), v], axis=0), v)
            return 0

        lax.fori_loop(first, CHUNKS // 2, gram, 0)

        exchange = pltpu.make_async_remote_copy(
            src_ref=acc, dst_ref=peer.at[slot], send_sem=peer_send.at[slot], recv_sem=peer_recv.at[slot],
            device_id=partner, device_id_type=MESH,
        )
        exchange.start()

        @pl.when(idx < STEPS - 1)
        def _():
            t_copy(group - 1, 1 - slot).start()

        t_copy(group, slot).wait()
        exchange.wait()

        s_full = acc[pl.ds(0, COLS), :] + peer[slot, pl.ds(0, COLS), :]
        g_full = acc[pl.ds(COLS, GROUP), :] + peer[slot, pl.ds(COLS, GROUP), :]
        t_mat = t_buf[slot]
        for width in (BLK, 2 * BLK, 4 * BLK):
            mask = (row // (2 * width) == column // (2 * width)) & (row // width < column // width)
            t_mat = t_mat - nn(nn(t_mat, jnp.where(mask, g_full, 0.0)), t_mat)
        w_full = nt(s_full, t_mat)

        def update(w, _):
            delta = nn(w_full, tile(w))
            out_ref[2 * w] -= delta[:, :LANES]
            out_ref[2 * w + 1] -= delta[:, LANES:]
            return 0

        lax.fori_loop(first, CHUNKS // 2, update, 0)
        return 0

    lax.fori_loop(0, STEPS, step, 0)


def gather_panels(v):
    return pl.pallas_call(
        gather_kernel,
        out_shape=jax.ShapeDtypeStruct((SLOTS, SIDE, SIDE, SIDE, BLK, LANES), jnp.float32),
        in_specs=[pl.BlockSpec(memory_space=pl.ANY)],
        out_specs=pl.BlockSpec(memory_space=pl.ANY),
        scratch_shapes=[
            pltpu.VMEM((SLOTS, SIDE, SIDE, SIDE, BLK, LANES), jnp.float32),
            pltpu.SemaphoreType.DMA((len(SEMS),)),
            pltpu.SemaphoreType.DMA((len(SEMS),)),
            pltpu.SemaphoreType.DMA((ROUNDS,)),
        ],
        compiler_params=pltpu.CompilerParams(collective_id=0, has_side_effects=True, vmem_limit_bytes=60 * 1024 * 1024),
        name="gather_panels",
    )(v)


def apply_panels(z, v, t):
    return pl.pallas_call(
        apply_kernel,
        out_shape=jax.ShapeDtypeStruct(z.shape, jnp.float32),
        in_specs=[
            pl.BlockSpec(memory_space=pltpu.VMEM),
            pl.BlockSpec(memory_space=pl.ANY),
            pl.BlockSpec(memory_space=pl.ANY),
        ],
        out_specs=pl.BlockSpec(memory_space=pltpu.VMEM),
        scratch_shapes=[
            pltpu.VMEM((SLOTS, SIDE, SIDE, SIDE, BLK, LANES), jnp.float32),
            pltpu.VMEM((COLS + GROUP, GROUP), jnp.float32),
            pltpu.VMEM((2, COLS + GROUP, GROUP), jnp.float32),
            pltpu.VMEM((2, GROUP, GROUP), jnp.float32),
            pltpu.SemaphoreType.DMA((ROUNDS,)),
            pltpu.SemaphoreType.DMA((2,)),
            pltpu.SemaphoreType.DMA((2,)),
            pltpu.SemaphoreType.DMA((2,)),
        ],
        compiler_params=pltpu.CompilerParams(collective_id=1, has_side_effects=True, vmem_limit_bytes=60 * 1024 * 1024),
        name="apply_panels",
    )(z, v, t)


def solution(mesh):
    def local_run(z_cols, v_local, t_local):
        z = lax.all_to_all(z_cols, "row", 0, 1, tiled=True)
        z = z.reshape(CHUNKS, LANES, COLS).transpose(0, 2, 1)
        v = v_local.reshape(CHUNKS, LANES, ROUNDS, BLK).transpose(2, 0, 3, 1)
        blocks = GROUP // BLK
        same = jnp.eye(blocks, dtype=bool)[None, :, None, :, None]
        t = jnp.where(same, t_local.reshape(STEPS, blocks, BLK, 1, BLK), 0.0).reshape(STEPS, GROUP, GROUP)
        out = apply_panels(z, gather_panels(v), t)
        return out.transpose(0, 2, 1).reshape(CHUNKS * LANES, COLS)

    return jax.shard_map(
        local_run,
        mesh=mesh,
        in_specs=(P("kpt", ("col", "row")), P(("kpt", "row"), "col"), P("kpt", None, None)),
        out_specs=P(("kpt", "row"), "col"),
        check_vma=False,
    )
```

time: 3500 us -> 492 us (0.14)
  matrix products: 1590 us -> 0 us
  waiting for transfers between devices: 1180 us -> 0.79 us
  blocking collectives: 663 us -> 0 us
  Pallas kernels: 0 us -> 442 us
    dot_general x576 -> x0, matrix products: 1590 us -> none  [the longest x192 765 us: panel_step(): jnp.einsum('lb,lm->bm', panel, z_val, precision=PRECISE, preferred_elemen...]
    all_gather x3 -> x0, waiting for transfers between devices: 1180 us -> none  [group_step(): gathered = lax.all_gather(own_panel, 'col')]
    psum x192 -> x0, blocking collectives: 663 us -> none  [panel_step(): s_full = lax.psum(s_part, 'row')]
    pallas_call x0 -> x2, Pallas kernels: none -> 442 us  [the longest x1 241 us: apply_panels(): pl.pallas_call(apply_kernel, out_shape=jax.ShapeDtypeStruct(z.shape, jnp....]
  transfers between devices with their start and end apart: 4 -> 1, of which waited for: 3 -> 1; matrix products, arithmetic and copies ran while one was open for 0% -> 0% of each run, Pallas kernels for 0% -> 0%
where the time goes in v1:
time: 492 us; the launch traced here: 491 us
  Pallas kernels  442 us (90%)
  local copies, waits for them, and re-layouts  36.7 us (7%)
  other arithmetic  6.25 us (1%)
    pallas_call x1, Pallas kernels, apply_panels(): pl.pallas_call(apply_kernel, out_shape=jax.ShapeDtypeStruct(z.shape, jnp....  241 us
    pallas_call x1, Pallas kernels, gather_panels(): pl.pallas_call(gather_kernel, out_shape=jax.ShapeDtypeStruct((SLOTS, SIDE...  201 us
    broadcast_in_dim x4, local copies, waits for them, and re-layouts, local_run(): jnp.where(same, t_local.reshape(STEPS, blocks, BLK, 1, BLK), 0.0)  26.9 us
  transfers between devices with their start and end apart: 1, of which 1 were waited for; matrix products, arithmetic and copies ran while one was open for 0% of the time, Pallas kernels for 0%

profile of v1, /device:TPU:1, one launch (start us, length us, event | category | flops | bytes accessed | tf_op | source)
XLA Modules:
  0.0 491.2 jit_solution(8310351018018656986)
XLA Ops:
  0.0 0.0 copy-start
  0.0 2.2 copy.19
  2.2 4.9 all-to-all-start
  7.1 0.1 broadcast_in_dim.29
  7.2 0.4 broadcast_in_dim.30
  7.6 0.8 all-to-all-done
  8.4 0.1 copy.12
  8.5 1.0 copy.20
  9.6 0.0 copy-done
  9.6 0.2 copy.13
  9.8 1.2 copy.18
  11.0 2.9 copy.8
  14.0 8.6 %broadcast_in_dim.33 = f32[24,8,32,8,32]{4,3,2,1,0:T(8,128)} broadcast(f32[24,8,32,32]{3,2,1,0:T(8,128)S(1)} %bitcast.32), dimensions={0,1,2,4} | broadcast | bytes 7077888 | tf_op jit(solution)/shard_map/jit(_where)/broadcast_in_dim | solution.py:318
  22.5 17.9 %broadcast_in_dim.34 = f32[24,256,256]{2,1,0:T(8,128)} reshape(f32[24,8,32,8,32]{4,3,2,1,0:T(8,128)} %broadcast_in_dim.33) | data formatting | bytes 12582912 | tf_op jit(solution)/shard_map/jit(_where)/broadcast_in_dim | solution.py:318
  40.4 201.4 %gather_panels.1.v_ref = f32[48,4,4,4,32,128]{5,4,3,2,1,0:T(8,128)} custom-call(f32[3,24,32,128]{3,2,1,0:T(8,128)} %bitcast.33), custom_call_target="tpu_custom_call" | custom-call | tf_op jit(solution)/shard_map/gather_panels/pallas_call | solution.py:270
  241.8 6.2 %broadcast_select_fusion.t_ref = f32[24,256,256]{2,1,0:T(8,128)} fusion(f32[24,256,256]{2,1,0:T(8,128)} %broadcast_in_dim.34, pred[256,256]{1,0:T(8,128)(4,1)S(1)} %broadcast_in_dim.30), kind=kLoop, calls=%fused_computation | loop fusion | flops 1572864 | bytes 12648448 | tf_op jit(solution)/shard_map/jit(_where)/select_n | solution.py:318
  248.0 241.1 %apply_panels.1 = f32[24,64,128]{2,1,0:T(8,128)} custom-call(f32[24,64,128]{2,1,0:T(8,128)} %bitcast.35, f32[48,4,4,4,32,128]{5,4,3,2,1,0:T(8,128)} %gather_panels.1.v_ref, f32[24,256,256]{2,1,0:T(8,128)} %broadcast_select_fusion.t_ref), custom_call_target="tpu_custom_call" | custom-call | tf_op jit(solution)/shard_map/apply_panels/pallas_call | solution.py:287
  489.1 2.1 copy_bitcast_fusion.1
  (1 shorter events, 0.0 us)
Async XLA Ops:
  0.0 9.6 %copy-start = (f32[3072,96]{0,1:T(8,128)S(1)}, f32[3072,96]{0,1:T(8,128)}, u32[]{:S(2)}) copy-start(f32[3072,96]{0,1:T(8,128)} %param.4) | copy-start | bytes 3538948
  2.2 6.2 %all-to-all-start = ((f32[2,3072,32]{1,2,0:T(8,128)}), f32[2,3072,32]{1,2,0:T(8,128)S(1)}, u32[]{:S(2)}, u32[]{:S(2)}) async-start(f32[2,3072,32]{1,2,0:T(8,128)} %bitcast.30), calls=%async_computation | async-start | bytes 1572864 | tf_op jit(solution)/shard_map/all_to_all | solution.py:313

commit v2 on v1

--- a/solution.py
+++ b/solution.py
@@ -117,8 +117,8 @@
         for kind, source in (("F+", -2), ("F-", 2)):
             self.each(rnd, colour, phase, kind, source, lambda copy: copy.wait_recv())
 
-    def event(self, name, rnd):
-        for colour in range(3):
+    def event(self, name, rnd, colours):
+        for colour in colours:
             if name == "A1":
                 self.start_own(rnd, colour, 0)
             elif name in ("F1", "F2", "F3"):
@@ -137,11 +137,16 @@
                         self.each(rnd, colour, phase, kind, source, lambda copy: copy.wait_send())
 
 
-EVENTS = (
-    ("A1", 2), ("A1", 1), ("A1", 0), ("F1", 2), ("A2", 2), ("F1", 1), ("F2", 2), ("A3", 2),
-    ("A2", 1), ("F1", 0), ("F3", 2), ("F2", 1), ("A2", 0), ("A3", 1), ("F2", 0), ("F3", 1),
-    ("A3", 0), ("D", 2), ("D", 1), ("F3", 0), ("D", 0),
+ALL = (0, 1, 2)
+OPENING = (
+    ("A1", 2, ALL), ("A1", 1, ALL), ("A1", 0, ALL), ("F1", 2, ALL), ("A2", 2, ALL), ("F2", 2, ALL), ("A3", 2, ALL),
+    ("F1", 1, ALL), ("A2", 1, ALL), ("F1", 0, ALL), ("F3", 2, ALL), ("F2", 1, ALL), ("A3", 1, ALL), ("A2", 0, ALL),
+    ("D", 2, ALL),
 )
+BEFORE_STEP = {
+    1: (("F2", 0, ALL),), 3: (("F3", 1, ALL),), 4: (("A3", 0, ALL),), 8: (("D", 1, ALL),), 12: (("F3", 0, ALL),),
+    16: (("D", 0, ALL),),
+}
 
 
 def nt(lhs, rhs):
@@ -152,19 +157,16 @@
     return lax.dot_general(lhs, rhs, (((1,), (0,)), ((), ())), precision=PRECISE, preferred_element_type=jnp.float32)
 
 
-def enter(gather, partner):
-    barrier = pltpu.get_barrier_semaphore()
-    peers = [] if gather is None else [gather.neighbour(axis, offset) for axis in "xyz" for offset in (1, -1)]
-    for peer in peers + ([] if partner is None else [partner]):
-        pl.semaphore_signal(barrier, inc=1, device_id=peer, device_id_type=MESH)
-    pl.semaphore_wait(barrier, len(peers) + (partner is not None))
-
-
-def gather_kernel(v_ref, out_ref, buf, send_sems, recv_sems, own_sems):
+def kernel(
+    z_ref, v_ref, t_ref, out_ref, buf, acc, peer, t_buf,
+    send_sems, recv_sems, own_sems, z_sems, peer_send, peer_recv, t_sems,
+):
     gather = Gather(buf, send_sems, recv_sems)
-    me = gather.me
+    me, core = gather.me, gather.core
+    partner = (gather.kpt, lax.axis_index("col"), 1 - core)
+
     own = []
-    for rnd in range(ROUNDS):
+    for rnd in reversed(range(ROUNDS)):
         copy = pltpu.make_async_copy(
             v_ref.at[rnd, pl.ds(8 * rnd, CHUNKS - 8 * rnd)],
             buf.at[pl.ds(ROUND_BASE[rnd], CHUNKS - 8 * rnd), me["z"], me["y"], me["x"]],
@@ -172,28 +174,30 @@
         )
         copy.start()
         own.append(copy)
-    enter(gather, None)
+    mine = pl.ds(core * (COLS // 2), COLS // 2)
+    z_keep = pltpu.make_async_copy(z_ref.at[core], out_ref.at[:, mine, :], z_sems.at[0])
+    z_keep.start()
+
+    barrier = pltpu.get_barrier_semaphore()
+    for axis in "xyz":
+        for offset in (1, -1):
+            pl.semaphore_signal(barrier, inc=1, device_id=gather.neighbour(axis, offset), device_id_type=MESH)
+    pl.semaphore_signal(barrier, inc=1, device_id=partner, device_id_type=MESH)
+    pl.semaphore_wait(barrier, 7)
+
     for copy in own:
         copy.wait()
-    for name, rnd in EVENTS:
-        gather.event(name, rnd)
-    gather.drain()
-    whole = pltpu.make_async_copy(buf, out_ref, own_sems.at[0])
-    whole.start()
-    whole.wait()
-
-
-def apply_kernel(z_ref, v_ref, t_ref, out_ref, buf, acc, peer, t_buf, v_sems, peer_send, peer_recv, t_sems):
-    partner = (lax.axis_index("kpt"), lax.axis_index("col"), 1 - lax.axis_index("row"))
-
-    def v_copy(rnd):
-        block = pl.ds(ROUND_BASE[rnd], CHUNKS - 8 * rnd)
-        return pltpu.make_async_copy(v_ref.at[block], buf.at[block], v_sems.at[rnd])
-
-    for rnd in reversed(range(ROUNDS)):
-        v_copy(rnd).start()
-    enter(None, partner)
-    out_ref[...] = z_ref[...]
+    for event in OPENING[:3]:
+        gather.event(*event)
+    z_give = pltpu.make_async_remote_copy(
+        src_ref=z_ref.at[1 - core], dst_ref=out_ref.at[:, mine, :], send_sem=z_sems.at[1], recv_sem=z_sems.at[2],
+        device_id=partner, device_id_type=MESH,
+    )
+    z_give.start()
+    for event in OPENING[3:]:
+        gather.event(*event)
+    z_keep.wait()
+    z_give.wait()
 
     row = lax.broadcasted_iota(jnp.int32, (GROUP, GROUP), 0)
     column = lax.broadcasted_iota(jnp.int32, (GROUP, GROUP), 1)
@@ -204,8 +208,11 @@
     t_copy(STEPS - 1, 0).start()
 
     def step(idx, _):
-        for rnd_needed in range(ROUNDS):
-            pl.when(idx == 16 - 8 * rnd_needed)(lambda rnd_needed=rnd_needed: v_copy(rnd_needed).wait())
+        for at, events in BEFORE_STEP.items():
+            @pl.when(idx == at)
+            def _(events=events):
+                for event in events:
+                    gather.event(*event)
 
         group = STEPS - 1 - idx
         rnd = group // 8
@@ -248,7 +255,10 @@
 
         s_full = acc[pl.ds(0, COLS), :] + peer[slot, pl.ds(0, COLS), :]
         g_full = acc[pl.ds(COLS, GROUP), :] + peer[slot, pl.ds(COLS, GROUP), :]
-        t_mat = t_buf[slot]
+        compact = t_buf[slot]
+        t_mat = jnp.where(
+            row // BLK == column // BLK, jnp.concatenate([compact] * (GROUP // BLK), axis=1), 0.0
+        )
         for width in (BLK, 2 * BLK, 4 * BLK):
             mask = (row // (2 * width) == column // (2 * width)) & (row // width < column // width)
             t_mat = t_mat - nn(nn(t_mat, jnp.where(mask, g_full, 0.0)), t_mat)
@@ -264,59 +274,38 @@
         return 0
 
     lax.fori_loop(0, STEPS, step, 0)
-
-
-def gather_panels(v):
-    return pl.pallas_call(
-        gather_kernel,
-        out_shape=jax.ShapeDtypeStruct((SLOTS, SIDE, SIDE, SIDE, BLK, LANES), jnp.float32),
-        in_specs=[pl.BlockSpec(memory_space=pl.ANY)],
-        out_specs=pl.BlockSpec(memory_space=pl.ANY),
-        scratch_shapes=[
-            pltpu.VMEM((SLOTS, SIDE, SIDE, SIDE, BLK, LANES), jnp.float32),
-            pltpu.SemaphoreType.DMA((len(SEMS),)),
-            pltpu.SemaphoreType.DMA((len(SEMS),)),
-            pltpu.SemaphoreType.DMA((ROUNDS,)),
-        ],
-        compiler_params=pltpu.CompilerParams(collective_id=0, has_side_effects=True, vmem_limit_bytes=60 * 1024 * 1024),
-        name="gather_panels",
-    )(v)
+    gather.drain()
 
 
 def apply_panels(z, v, t):
     return pl.pallas_call(
-        apply_kernel,
-        out_shape=jax.ShapeDtypeStruct(z.shape, jnp.float32),
-        in_specs=[
-            pl.BlockSpec(memory_space=pltpu.VMEM),
-            pl.BlockSpec(memory_space=pl.ANY),
-            pl.BlockSpec(memory_space=pl.ANY),
-        ],
+        kernel,
+        out_shape=jax.ShapeDtypeStruct((CHUNKS, COLS, LANES), jnp.float32),
+        in_specs=[pl.BlockSpec(memory_space=pl.ANY)] * 3,
         out_specs=pl.BlockSpec(memory_space=pltpu.VMEM),
         scratch_shapes=[
             pltpu.VMEM((SLOTS, SIDE, SIDE, SIDE, BLK, LANES), jnp.float32),
             pltpu.VMEM((COLS + GROUP, GROUP), jnp.float32),
             pltpu.VMEM((2, COLS + GROUP, GROUP), jnp.float32),
-            pltpu.VMEM((2, GROUP, GROUP), jnp.float32),
+            pltpu.VMEM((2, GROUP, BLK), jnp.float32),
+            pltpu.SemaphoreType.DMA((len(SEMS),)),
+            pltpu.SemaphoreType.DMA((len(SEMS),)),
             pltpu.SemaphoreType.DMA((ROUNDS,)),
+            pltpu.SemaphoreType.DMA((3,)),
             pltpu.SemaphoreType.DMA((2,)),
             pltpu.SemaphoreType.DMA((2,)),
             pltpu.SemaphoreType.DMA((2,)),
         ],
-        compiler_params=pltpu.CompilerParams(collective_id=1, has_side_effects=True, vmem_limit_bytes=60 * 1024 * 1024),
+        compiler_params=pltpu.CompilerParams(collective_id=0, has_side_effects=True, vmem_limit_bytes=60 * 1024 * 1024),
         name="apply_panels",
     )(z, v, t)
 
 
 def solution(mesh):
     def local_run(z_cols, v_local, t_local):
-        z = lax.all_to_all(z_cols, "row", 0, 1, tiled=True)
-        z = z.reshape(CHUNKS, LANES, COLS).transpose(0, 2, 1)
+        z = z_cols.reshape(2, CHUNKS, LANES, COLS // 2).transpose(0, 1, 3, 2)
         v = v_local.reshape(CHUNKS, LANES, ROUNDS, BLK).transpose(2, 0, 3, 1)
-        blocks = GROUP // BLK
-        same = jnp.eye(blocks, dtype=bool)[None, :, None, :, None]
-        t = jnp.where(same, t_local.reshape(STEPS, blocks, BLK, 1, BLK), 0.0).reshape(STEPS, GROUP, GROUP)
-        out = apply_panels(z, gather_panels(v), t)
+        out = apply_panels(z, v, t_local.reshape(STEPS, GROUP, BLK))
         return out.transpose(0, 2, 1).reshape(CHUNKS * LANES, COLS)
 
     return jax.shard_map(

time: 492 us -> 334 us (0.68)
  the two profiles are of different devices: /device:TPU:1 before, /device:TPU:97 now
where the time goes in v2:
time: 334 us; the launch traced here: 333 us
  Pallas kernels  324 us (97%)
  local copies, waits for them, and re-layouts  9.21 us (3%)
    pallas_call x1, Pallas kernels, apply_panels(): pl.pallas_call(kernel, out_shape=jax.ShapeDtypeStruct((CHUNKS, COLS, LANE...  324 us

profile of v2, /device:TPU:97, one launch (start us, length us, event | category | flops | bytes accessed | tf_op | source)
XLA Modules:
  0.0 333.5 jit_solution(16456736081544053966)
XLA Ops:
  0.0 1.3 copy.10
  1.3 0.0 copy-start
  1.3 1.1 copy.16
  2.4 0.4 copy-done
  2.8 0.2 copy.11
  3.0 0.0 copy-start.1
  3.0 1.2 copy.15
  4.2 0.2 copy-done.1
  4.4 2.8 copy.7
  7.2 324.2 %apply_panels.1 = f32[24,64,128]{2,1,0:T(8,128)} custom-call(f32[2,24,32,128]{3,2,1,0:T(8,128)} %bitcast.27, f32[3,24,32,128]{3,2,1,0:T(8,128)} %bitcast.25, f32[24,256,32]{2,1,0:T(8,128)} %bitcast.23), custom_call_target="tpu_custom_call" | custom-call | tf_op jit(solution)/shard_map/apply_panels/pallas_call | solution.py:281
  331.4 2.1 copy_bitcast_fusion.1
Async XLA Ops:
  1.3 1.5 copy-start
  3.0 1.4 copy-start.1

commit v3 on v2

v3 whole, which is shorter than its diff:
```python
import jax
import jax.numpy as jnp
from jax import lax
from jax.experimental import pallas as pl
from jax.experimental.pallas import tpu as pltpu
from jax.sharding import PartitionSpec as P

PRECISE = lax.Precision.HIGHEST
MESH = pl.DeviceIdType.MESH

SIDE = 4
BLK = 32
ROUNDS = 3
LANES = 128
CHUNKS = 24
GROUP = 256
STEPS = 24
COLS = 64

ORDER = (("x", "y", "z"), ("y", "z", "x"), ("z", "x", "y"))
SHARES = {
    24: (8, 8, 8), 22: (8, 7, 7), 20: (7, 7, 6), 18: (6, 6, 6),
    16: (5, 5, 6), 14: (5, 5, 4), 12: (4, 4, 4), 10: (3, 3, 4),
    8: (3, 3, 2), 6: (2, 2, 2), 4: (1, 1, 2), 2: (1, 1, 0),
}
ROUND_BASE = (0, 24, 40)
SLOTS = 48
KINDS = ("A+", "A-", "F+", "F-")
FACTOR = 3
OCTET = 8
SHARE = 16


def axes_of(rnd, colour):
    return ORDER[rnd if colour == FACTOR else colour]


def part(rnd, z_src, colour):
    first = 8 * rnd + 2 * z_src
    shares = SHARES[CHUNKS - first]
    return ROUND_BASE[rnd] + first - 8 * rnd + sum(shares[:colour]), shares[colour]


def sem_table():
    table = {}
    for rnd in range(ROUNDS):
        for colour in range(4):
            for phase in range(3):
                planes = range(SIDE) if colour != FACTOR and "z" in ORDER[colour][:phase] else (None,)
                for kind in KINDS:
                    for plane in planes:
                        table[rnd, colour, phase, kind, plane] = len(table)
    return table


SEMS = sem_table()


class Gather:
    def __init__(self, buf, factors, send_sems, recv_sems):
        col = lax.axis_index("col")
        self.kpt, self.core = lax.axis_index("kpt"), lax.axis_index("row")
        self.me = {"z": col // 16, "y": (col // 4) % 4, "x": col % 4}
        self.buf, self.factors, self.send_sems, self.recv_sems = buf, factors, send_sems, recv_sems
        self.at = {(axis, offset): (self.me[axis] + offset) % SIDE for axis in "xyz" for offset in (1, 2, 3)}
        self.peer = {(axis, offset): self.find(axis, offset) for axis in "xyz" for offset in (1, 3)}

    def find(self, axis, offset):
        at = dict(self.me)
        at[axis] = self.at[axis, offset]
        return (self.kpt, at["z"] * 16 + at["y"] * 4 + at["x"], self.core)

    def shifted(self, axis, offset):
        return self.me[axis] if offset == 0 else self.at[axis, offset % SIDE]

    def neighbour(self, axis, offset):
        return self.peer[axis, offset % SIDE]

    def each(self, rnd, colour, phase, kind, source, fn, planes=None):
        axis = axes_of(rnd, colour)[phase]
        whole = axes_of(rnd, colour)[:phase]
        rows = {"A+": pl.ds(0, BLK), "A-": pl.ds(0, BLK), "F+": pl.ds(0, BLK // 2), "F-": pl.ds(BLK // 2, BLK // 2)}[kind]
        target = self.neighbour(axis, 1 if kind[1] == "+" else -1)

        def coordinate(name):
            if name in whole:
                return slice(None)
            return self.shifted(name, source) if name == axis else self.me[name]

        def send(block, sem):
            fn(
                pltpu.make_async_remote_copy(
                    src_ref=block, dst_ref=block,
                    send_sem=self.send_sems.at[sem], recv_sem=self.recv_sems.at[sem],
                    device_id=target, device_id_type=MESH,
                )
            )

        def panels(plane, sem):
            slot, count = part(rnd, plane, colour)
            if count:
                send(self.buf.at[pl.ds(slot, count), plane, coordinate("y"), coordinate("x"), rows, :], sem)

        if colour == FACTOR:
            block = self.factors.at[self.core, rnd, coordinate("z"), coordinate("y"), coordinate("x"), rows, :]
            send(block, SEMS[rnd, colour, phase, kind, None])
        elif "z" in whole:
            for plane in reversed(range(SIDE)) if planes is None else planes:
                panels(plane, SEMS[rnd, colour, phase, kind, plane])
        else:
            plane_here = self.shifted("z", source) if axis == "z" else self.me["z"]
            for plane in range(SIDE):
                pl.when(plane_here == plane)(
                    lambda plane=plane: panels(plane, SEMS[rnd, colour, phase, kind, None])
                )

    def start_own(self, rnd, colour, phase):
        for kind in ("A+", "A-"):
            self.each(rnd, colour, phase, kind, 0, lambda copy: copy.start())

    def forward(self, rnd, colour, phase, planes=None):
        for kind, relay, source in (("A+", "F+", -1), ("A-", "F-", 1)):
            self.each(rnd, colour, phase, kind, source, lambda copy: copy.wait_recv(), planes)
            self.each(rnd, colour, phase, relay, source, lambda copy: copy.start(), planes)

    def finish(self, rnd, colour, phase, planes=None):
        for kind, source in (("F+", -2), ("F-", 2)):
            self.each(rnd, colour, phase, kind, source, lambda copy: copy.wait_recv(), planes)

    def event(self, name, rnd, colours, planes=None):
        for colour in colours:
            if name == "A1":
                self.start_own(rnd, colour, 0)
            elif name in ("F1", "F2", "F3"):
                self.forward(rnd, colour, int(name[1]) - 1, planes)
            elif name in ("A2", "A3"):
                self.finish(rnd, colour, int(name[1]) - 2)
                self.start_own(rnd, colour, int(name[1]) - 1)
            else:
                self.finish(rnd, colour, 2, planes)

    def drain(self):
        for rnd in range(ROUNDS):
            for colour in range(4):
                for phase in range(3):
                    for kind, source in (("A+", 0), ("A-", 0), ("F+", -1), ("F-", 1)):
                        self.each(rnd, colour, phase, kind, source, lambda copy: copy.wait_send())


ALL = (0, 1, 2)
T = (FACTOR,)
AFTER_SPREAD = (("A1", 2, ALL), ("A1", 1, ALL))
AFTER_GRAM = (("F1", 2, ALL),)
AFTER_PAIR = (("A2", 2, ALL),)
AFTER_SUM = (("F2", 2, ALL), ("F1", 1, ALL))
AFTER_GRAMS = (("A3", 2, ALL), ("A1", 0, ALL), ("A2", 1, ALL))
AFTER_FACTORS = (
    ("A1", 2, T), ("A1", 1, T), ("A1", 0, T), ("F1", 2, T), ("F1", 1, T), ("F1", 0, T),
    ("A2", 2, T), ("A2", 1, T), ("A2", 0, T), ("F1", 0, ALL), ("F3", 2, ALL), ("F2", 1, ALL),
    ("F2", 2, T), ("F2", 1, T), ("F2", 0, T), ("A3", 2, T), ("A3", 1, T), ("A3", 0, T), ("A3", 1, ALL),
    ("A2", 0, ALL), ("F3", 2, T), ("F3", 1, T), ("F3", 0, T), ("D", 2, ALL), ("D", 2, T), ("D", 1, T), ("D", 0, T),
)
BEFORE_STEP = {
    2: (("F2", 0, ALL),), 5: (("F3", 1, ALL), ("A3", 0, ALL)), 8: (("D", 1, ALL),),
    14: (("F3", 0, ALL),), 16: (("D", 0, ALL),),
}


def nt(lhs, rhs):
    return lax.dot_general(lhs, rhs, (((1,), (1,)), ((), ())), precision=PRECISE, preferred_element_type=jnp.float32)


def nn(lhs, rhs):
    return lax.dot_general(lhs, rhs, (((1,), (0,)), ((), ())), precision=PRECISE, preferred_element_type=jnp.float32)


def merge_factors(t, grams):
    row = lax.broadcasted_iota(jnp.int32, (GROUP, GROUP), 0)
    column = lax.broadcasted_iota(jnp.int32, (GROUP, GROUP), 1)
    for width in (BLK, 2 * BLK, 4 * BLK):
        above = (row // (2 * width) == column // (2 * width)) & (row // width < column // width)
        left = [nn(t_mat, jnp.where(above, gram, 0.0)) for t_mat, gram in zip(t, grams)]
        t = [t_mat - nn(half, t_mat) for t_mat, half in zip(t, left)]
    return t


def kernel(
    z_ref, v_ref, octet_ref, t_ref, out_ref, buf, factors, acc, peer, t_buf, rows_buf, gram, gram_peer, gram_pair,
    gram_parts, gram_full,
    send_sems, recv_sems, own_sems, z_sems, peer_send, peer_recv, octet_send, octet_recv, pair_send, pair_recv,
):
    gather = Gather(buf, factors, send_sems, recv_sems)
    me, core = gather.me, gather.core
    col = lax.axis_index("col")
    partner = (gather.kpt, col, 1 - core)
    seat = col % OCTET
    mates = {hop: (seat + hop) % OCTET for hop in range(1, OCTET)}

    def mate(hop):
        return (gather.kpt, col - seat + mates[hop], core)

    def to_mate(stage, hop, source, target):
        sem = stage * OCTET + hop
        return pltpu.make_async_remote_copy(
            src_ref=source, dst_ref=target, send_sem=octet_send.at[sem], recv_sem=octet_recv.at[sem],
            device_id=mate(hop), device_id_type=MESH,
        )

    def to_partner(sem, source, target):
        return pltpu.make_async_remote_copy(
            src_ref=source, dst_ref=target, send_sem=pair_send.at[sem], recv_sem=pair_recv.at[sem],
            device_id=partner, device_id_type=MESH,
        )

    own = [
        pltpu.make_async_copy(v_ref, buf.at[:, me["z"], me["y"], me["x"]], own_sems.at[0]),
        pltpu.make_async_copy(octet_ref.at[:, seat], rows_buf.at[:, seat], own_sems.at[1]),
    ]
    for rnd in range(ROUNDS):
        own.append(pltpu.make_async_copy(t_ref.at[8 * rnd + col // OCTET], t_buf.at[rnd], own_sems.at[2 + rnd]))
    for copy in own:
        copy.start()
    mine = pl.ds(core * (COLS // 2), COLS // 2)
    z_keep = pltpu.make_async_copy(z_ref.at[core], out_ref.at[:, mine, :], z_sems.at[0])
    z_keep.start()

    barrier = pltpu.get_barrier_semaphore()
    peers = [gather.neighbour(axis, offset) for axis in "xyz" for offset in (1, -1)]
    peers += [mate(hop) for hop in mates] + [partner]
    for device in peers:
        pl.semaphore_signal(barrier, inc=1, device_id=device, device_id_type=MESH)
    pl.semaphore_wait(barrier, len(peers))

    def run(events):
        for event in events:
            gather.event(*event)

    spread = [to_mate(0, hop, octet_ref.at[:, at], rows_buf.at[:, seat]) for hop, at in mates.items()]
    for copy in spread:
        copy.start()
    for copy in own:
        copy.wait()
    run(AFTER_SPREAD)
    z_give = pltpu.make_async_remote_copy(
        src_ref=z_ref.at[1 - core], dst_ref=out_ref.at[:, mine, :], send_sem=z_sems.at[1], recv_sem=z_sems.at[2],
        device_id=partner, device_id_type=MESH,
    )
    z_give.start()
    for copy in spread:
        copy.wait()
    for rnd, chunks in enumerate(((0, 1, 2), (3, 4), (5,))):
        panel = jnp.concatenate([rows_buf[chunk].reshape(GROUP, LANES) for chunk in chunks], axis=1)
        gram[:, :, rnd] = nt(panel, panel).reshape(OCTET, 2, SHARE, GROUP)
    pair = to_partner(0, gram.at[:, 1 - core], gram_peer)
    pair.start()
    run(AFTER_GRAM)
    pair.wait()
    gram_pair[...] = gram[:, core] + gram_peer[...]
    scatter = [to_mate(1, hop, gram_pair.at[at], gram_parts.at[seat]) for hop, at in mates.items()]
    for copy in scatter:
        copy.start()
    gram_parts[seat] = gram_pair[seat]
    run(AFTER_PAIR)
    for copy in scatter:
        copy.wait()
    gram_full[core, seat] = jnp.sum(gram_parts[...], axis=0)
    collect = [to_mate(2, hop, gram_full.at[core, seat], gram_full.at[core, seat]) for hop in mates]
    for copy in collect:
        copy.start()
    run(AFTER_SUM)
    for copy in collect:
        copy.wait()
    pair = to_partner(1, gram_full.at[core], gram_full.at[core])
    pair.start()
    run(AFTER_GRAMS)
    pair.wait()

    row = lax.broadcasted_iota(jnp.int32, (GROUP, GROUP), 0)
    column = lax.broadcasted_iota(jnp.int32, (GROUP, GROUP), 1)
    blocks = [
        jnp.where(row // BLK == column // BLK, jnp.concatenate([t_buf[rnd]] * OCTET, axis=1), 0.0)
        for rnd in range(ROUNDS)
    ]
    grams = [
        jnp.concatenate([gram_full[half, at, rnd] for at in range(OCTET) for half in range(2)], axis=0)
        for rnd in range(ROUNDS)
    ]
    for rnd, t_mat in enumerate(merge_factors(blocks, grams)):
        for half in range(2):
            rows_buf[2 * rnd + half] = t_mat[:, half * LANES : (half + 1) * LANES].reshape(OCTET, BLK, LANES)
        factors[core, rnd, me["z"], me["y"], me["x"]] = rows_buf[2 * rnd + core, seat]
    run(AFTER_FACTORS)
    halves = [to_partner(2 + rnd, factors.at[core, rnd], factors.at[core, rnd]) for rnd in range(ROUNDS)]
    for copy in reversed(halves):
        copy.start()
    z_keep.wait()
    z_give.wait()
    for copy in halves:
        copy.wait()

    def step(idx, _):
        for at, events in BEFORE_STEP.items():
            @pl.when(idx == at)
            def _(events=events):
                for event in events:
                    gather.event(*event)

        group = STEPS - 1 - idx
        rnd = group // 8
        plane = (group % 8) // 2
        pair_row = (group % 2) * 2
        slot = idx % 2
        shift = 16 * rnd - 4 * rnd * (rnd - 1)
        first = 4 * rnd + plane

        def tile(w):
            halves = [
                buf[shift + 2 * w + half, plane, pl.ds(pair_row, 2), :, :, :].reshape(GROUP, LANES) for half in range(2)
            ]
            return jnp.concatenate(halves, axis=1)

        def z_tile(w):
            return jnp.concatenate([out_ref[2 * w], out_ref[2 * w + 1]], axis=1)

        acc[...] = jnp.zeros_like(acc)

        def project(w, _):
            acc[...] += nt(z_tile(w), tile(w))
            return 0

        lax.fori_loop(first, CHUNKS // 2, project, 0)

        exchange = pltpu.make_async_remote_copy(
            src_ref=acc, dst_ref=peer.at[slot], send_sem=peer_send.at[slot], recv_sem=peer_recv.at[slot],
            device_id=partner, device_id_type=MESH,
        )
        exchange.start()

        t_mat = jnp.concatenate(
            [factors[half, rnd, plane, pl.ds(pair_row, 2)].reshape(GROUP, LANES) for half in range(2)], axis=1
        )
        exchange.wait()
        w_full = nt(acc[...] + peer[slot], t_mat)

        def update(w, _):
            delta = nn(w_full, tile(w))
            out_ref[2 * w] -= delta[:, :LANES]
            out_ref[2 * w + 1] -= delta[:, LANES:]
            return 0

        lax.fori_loop(first, CHUNKS // 2, update, 0)
        return 0

    lax.fori_loop(0, STEPS, step, 0)
    gather.drain()


def apply_panels(z, v, t):
    def vmem(*shape):
        return pltpu.VMEM(shape, jnp.float32)

    return pl.pallas_call(
        kernel,
        out_shape=jax.ShapeDtypeStruct((CHUNKS, COLS, LANES), jnp.float32),
        in_specs=[pl.BlockSpec(memory_space=pl.ANY)] * 4,
        out_specs=pl.BlockSpec(memory_space=pltpu.VMEM),
        scratch_shapes=[
            vmem(SLOTS, SIDE, SIDE, SIDE, BLK, LANES),
            vmem(2, ROUNDS, SIDE, SIDE, SIDE, BLK, LANES),
            vmem(COLS, GROUP),
            vmem(2, COLS, GROUP),
            vmem(ROUNDS, GROUP, BLK),
            vmem(SLOTS // OCTET, OCTET, BLK, LANES),
            vmem(OCTET, 2, ROUNDS, SHARE, GROUP),
            vmem(OCTET, ROUNDS, SHARE, GROUP),
            vmem(OCTET, ROUNDS, SHARE, GROUP),
            vmem(OCTET, ROUNDS, SHARE, GROUP),
            vmem(2, OCTET, ROUNDS, SHARE, GROUP),
            pltpu.SemaphoreType.DMA((len(SEMS),)),
            pltpu.SemaphoreType.DMA((len(SEMS),)),
            pltpu.SemaphoreType.DMA((2 + ROUNDS,)),
            pltpu.SemaphoreType.DMA((3,)),
            pltpu.SemaphoreType.DMA((2,)),
            pltpu.SemaphoreType.DMA((2,)),
            pltpu.SemaphoreType.DMA((3 * OCTET,)),
            pltpu.SemaphoreType.DMA((3 * OCTET,)),
            pltpu.SemaphoreType.DMA((2 + ROUNDS,)),
            pltpu.SemaphoreType.DMA((2 + ROUNDS,)),
        ],
        compiler_params=pltpu.CompilerParams(collective_id=0, has_side_effects=True, vmem_limit_bytes=67043328),
        name="apply_panels",
    )(z, v, v.reshape(SLOTS // OCTET, OCTET, BLK, LANES), t)


def solution(mesh):
    def local_run(z_cols, v_local, t_local):
        z = z_cols.reshape(2, CHUNKS, LANES, COLS // 2).transpose(0, 1, 3, 2)
        v = v_local.reshape(CHUNKS, LANES, ROUNDS, BLK).transpose(2, 0, 3, 1)
        v = jnp.concatenate([v[rnd, 8 * rnd :] for rnd in range(ROUNDS)], axis=0)
        out = apply_panels(z, v, t_local.reshape(STEPS, GROUP, BLK))
        return out.transpose(0, 2, 1).reshape(CHUNKS * LANES, COLS)

    return jax.shard_map(
        local_run,
        mesh=mesh,
        in_specs=(P("kpt", ("col", "row")), P(("kpt", "row"), "col"), P("kpt", None, None)),
        out_specs=P(("kpt", "row"), "col"),
        check_vma=False,
    )
```

time: 334 us -> 308 us (0.922)
  the two profiles are of different devices: /device:TPU:97 before, /device:TPU:1 now
where the time goes in v3:
time: 308 us; the launch traced here: 307 us
  Pallas kernels  298 us (97%)
  local copies, waits for them, and re-layouts  8.59 us (3%)
    pallas_call x1, Pallas kernels, apply_panels(): pl.pallas_call(kernel, out_shape=jax.ShapeDtypeStruct((CHUNKS, COLS, LANE...  298 us

profile of v3, /device:TPU:1, one launch (start us, length us, event | category | flops | bytes accessed | tf_op | source)
XLA Modules:
  0.0 307.2 jit_solution(15473585329415091969)
XLA Ops:
  0.0 1.3 copy.10
  1.3 0.0 copy-start
  1.3 1.1 copy.16
  2.4 0.4 copy-done
  2.8 0.2 copy.11
  3.0 0.2 copy.15
  3.2 0.0 copy-start.1
  3.3 0.9 pad_maximum_fusion.v_ref
  4.2 0.5 copy-done.1
  4.7 2.8 copy.7
  7.5 297.6 %apply_panels.1 = f32[24,64,128]{2,1,0:T(8,128)} custom-call(f32[2,24,32,128]{3,2,1,0:T(8,128)} %bitcast.36, f32[48,32,128]{2,1,0:T(8,128)} %pad_maximum_fusion.v_ref, f32[6,8,32,128]{3,2,1,0:T(8,128)} %bitcast.31, f32[24,256,32]{2,1,0:T(8,128)} %bitcast.30), custom_call_target="tpu_custom_call" | custom-call | tf_op jit(solution)/shard_map/apply_panels/pallas_call | solution.py:362
  305.2 2.1 copy_bitcast_fusion.1
  (3 shorter events, 0.1 us)
Async XLA Ops:
  1.3 1.5 copy-start
  3.2 1.5 copy-start.1

commit v4 on v3

--- a/solution.py
+++ b/solution.py
@@ -19,10 +19,11 @@
 
 ORDER = (("x", "y", "z"), ("y", "z", "x"), ("z", "x", "y"))
 SHARES = {
-    24: (8, 8, 8), 22: (8, 7, 7), 20: (7, 7, 6), 18: (6, 6, 6),
-    16: (5, 5, 6), 14: (5, 5, 4), 12: (4, 4, 4), 10: (3, 3, 4),
-    8: (3, 3, 2), 6: (2, 2, 2), 4: (1, 1, 2), 2: (1, 1, 0),
+    24: (4, 10, 10), 22: (4, 9, 9), 20: (4, 8, 8), 18: (4, 7, 7),
+    16: (6, 5, 5), 14: (4, 5, 5), 12: (4, 4, 4), 10: (4, 3, 3),
+    8: (2, 3, 3), 6: (2, 2, 2), 4: (2, 1, 1), 2: (1, 0, 1),
 }
+ROWS_BASE = (0, 3, 5)
 ROUND_BASE = (0, 24, 40)
 SLOTS = 48
 KINDS = ("A+", "A-", "F+", "F-")
@@ -114,9 +115,9 @@
                     lambda plane=plane: panels(plane, SEMS[rnd, colour, phase, kind, None])
                 )
 
-    def start_own(self, rnd, colour, phase):
+    def start_own(self, rnd, colour, phase, planes=None):
         for kind in ("A+", "A-"):
-            self.each(rnd, colour, phase, kind, 0, lambda copy: copy.start())
+            self.each(rnd, colour, phase, kind, 0, lambda copy: copy.start(), planes)
 
     def forward(self, rnd, colour, phase, planes=None):
         for kind, relay, source in (("A+", "F+", -1), ("A-", "F-", 1)):
@@ -127,17 +128,21 @@
         for kind, source in (("F+", -2), ("F-", 2)):
             self.each(rnd, colour, phase, kind, source, lambda copy: copy.wait_recv(), planes)
 
-    def event(self, name, rnd, colours, planes=None):
-        for colour in colours:
-            if name == "A1":
-                self.start_own(rnd, colour, 0)
-            elif name in ("F1", "F2", "F3"):
-                self.forward(rnd, colour, int(name[1]) - 1, planes)
-            elif name in ("A2", "A3"):
-                self.finish(rnd, colour, int(name[1]) - 2)
-                self.start_own(rnd, colour, int(name[1]) - 1)
-            else:
-                self.finish(rnd, colour, 2, planes)
+    def event(self, name, rnd, colour, plane=None):
+        planes = None if plane is None else (plane,)
+        if name == "A1":
+            self.start_own(rnd, colour, 0)
+        elif name in ("F1", "F2", "F3"):
+            self.forward(rnd, colour, int(name[1]) - 1, planes)
+        elif name in ("A2", "A3"):
+            phase = int(name[1]) - 1
+            if planes is None or "z" in axes_of(rnd, colour)[: phase - 1]:
+                self.finish(rnd, colour, phase - 1, planes)
+            elif plane == SIDE - 1:
+                self.finish(rnd, colour, phase - 1)
+            self.start_own(rnd, colour, phase, planes)
+        else:
+            self.finish(rnd, colour, 2, planes)
 
     def drain(self):
         for rnd in range(ROUNDS):
@@ -147,22 +152,105 @@
                         self.each(rnd, colour, phase, kind, source, lambda copy: copy.wait_send())
 
 
-ALL = (0, 1, 2)
-T = (FACTOR,)
-AFTER_SPREAD = (("A1", 2, ALL), ("A1", 1, ALL))
-AFTER_GRAM = (("F1", 2, ALL),)
-AFTER_PAIR = (("A2", 2, ALL),)
-AFTER_SUM = (("F2", 2, ALL), ("F1", 1, ALL))
-AFTER_GRAMS = (("A3", 2, ALL), ("A1", 0, ALL), ("A2", 1, ALL))
-AFTER_FACTORS = (
-    ("A1", 2, T), ("A1", 1, T), ("A1", 0, T), ("F1", 2, T), ("F1", 1, T), ("F1", 0, T),
-    ("A2", 2, T), ("A2", 1, T), ("A2", 0, T), ("F1", 0, ALL), ("F3", 2, ALL), ("F2", 1, ALL),
-    ("F2", 2, T), ("F2", 1, T), ("F2", 0, T), ("A3", 2, T), ("A3", 1, T), ("A3", 0, T), ("A3", 1, ALL),
-    ("A2", 0, ALL), ("F3", 2, T), ("F3", 1, T), ("F3", 0, T), ("D", 2, ALL), ("D", 2, T), ("D", 1, T), ("D", 0, T),
+LOW, MID, TOP = range(ROUNDS)
+XYZ, YZX, ZXY = range(3)
+Z0, Z1, Z2, Z3 = range(SIDE)
+OPENING = (
+    (
+        ("A1", TOP, ZXY), ("A1", TOP, YZX), ("A1", TOP, XYZ), ("A1", LOW, XYZ), ("A1", MID, XYZ), ("A1", LOW, ZXY),
+        ("A1", MID, YZX), ("F1", TOP, YZX), ("F1", TOP, ZXY), ("A1", LOW, YZX), ("A1", MID, ZXY), ("F1", MID, YZX),
+        ("F1", LOW, XYZ), ("F1", LOW, ZXY), ("F1", TOP, XYZ), ("A2", TOP, ZXY, Z3), ("A2", TOP, YZX),
+        ("A2", TOP, ZXY, Z2), ("A2", TOP, ZXY, Z0), ("F1", MID, XYZ), ("A2", TOP, ZXY, Z1),
+    ),
+    (
+        ("F2", TOP, ZXY, Z3), ("A2", LOW, ZXY, Z3), ("A2", TOP, XYZ), ("A2", MID, YZX), ("F1", LOW, YZX),
+        ("A2", LOW, ZXY, Z1), ("F2", TOP, YZX),
+    ),
+    (
+        ("A2", MID, XYZ), ("F2", TOP, ZXY, Z1), ("F2", LOW, ZXY, Z3), ("F1", MID, ZXY), ("A2", LOW, ZXY, Z2),
+        ("A2", LOW, YZX),
+    ),
+    (
+        ("F2", TOP, XYZ), ("A3", TOP, ZXY, Z3),
+    ),
+    (
+        ("A3", TOP, YZX, Z3), ("A3", LOW, ZXY, Z3), ("A2", LOW, ZXY, Z0), ("A3", TOP, YZX, Z2), ("A2", MID, ZXY, Z3),
+        ("A2", MID, ZXY, Z0), ("A3", TOP, YZX, Z0), ("A2", MID, ZXY, Z2), ("F2", MID, YZX),
+    ),
+    (
+        ("F2", LOW, ZXY, Z0), ("A1", MID, FACTOR), ("A3", TOP, ZXY, Z1), ("A2", MID, ZXY, Z1), ("F2", TOP, ZXY, Z2),
+        ("F2", TOP, ZXY, Z0), ("A2", LOW, XYZ), ("A1", TOP, FACTOR), ("A3", TOP, XYZ), ("A3", MID, YZX, Z3),
+        ("A1", LOW, FACTOR), ("F1", TOP, FACTOR), ("A3", TOP, ZXY, Z2), ("F1", MID, FACTOR), ("A3", TOP, YZX, Z1),
+        ("F3", TOP, ZXY, Z1), ("F2", LOW, YZX), ("F3", TOP, ZXY, Z3), ("F3", TOP, YZX, Z0), ("A3", TOP, ZXY, Z0),
+        ("F2", MID, ZXY, Z3), ("A2", TOP, FACTOR), ("F3", TOP, YZX, Z2), ("F2", MID, ZXY, Z2), ("A2", MID, FACTOR),
+        ("F3", TOP, XYZ), ("F2", MID, ZXY, Z0), ("F1", LOW, FACTOR), ("F2", MID, XYZ), ("F3", MID, YZX, Z3),
+        ("F2", TOP, FACTOR), ("F3", TOP, YZX, Z3), ("A3", MID, ZXY, Z3), ("D", TOP, YZX, Z2), ("F3", TOP, YZX, Z1),
+        ("A3", MID, YZX, Z1), ("F2", MID, FACTOR), ("F3", TOP, ZXY, Z0), ("A3", MID, XYZ), ("D", TOP, XYZ),
+        ("A2", LOW, FACTOR), ("A3", TOP, FACTOR), ("F3", MID, ZXY, Z3), ("F2", MID, ZXY, Z1), ("D", TOP, ZXY, Z1),
+        ("A3", MID, YZX, Z2), ("D", TOP, YZX, Z0), ("D", MID, YZX, Z3), ("F2", LOW, FACTOR), ("A3", MID, FACTOR),
+        ("A3", MID, YZX, Z0), ("D", TOP, YZX, Z1), ("F3", TOP, FACTOR), ("F3", TOP, ZXY, Z2), ("A3", MID, ZXY, Z1),
+        ("F3", MID, FACTOR), ("F3", MID, YZX, Z2), ("D", TOP, ZXY, Z3), ("F2", LOW, XYZ), ("D", TOP, YZX, Z3),
+        ("D", TOP, FACTOR), ("D", TOP, ZXY, Z0), ("A3", MID, ZXY, Z2), ("F3", MID, ZXY, Z1), ("F2", LOW, ZXY, Z2),
+        ("A3", LOW, FACTOR), ("D", TOP, ZXY, Z2),
+    ),
 )
 BEFORE_STEP = {
-    2: (("F2", 0, ALL),), 5: (("F3", 1, ALL), ("A3", 0, ALL)), 8: (("D", 1, ALL),),
-    14: (("F3", 0, ALL),), 16: (("D", 0, ALL),),
+    1: (
+        ("F3", MID, XYZ), ("D", MID, ZXY, Z3),
+    ),
+    3: (
+        ("F3", MID, YZX, Z1), ("D", MID, FACTOR),
+    ),
+    4: (
+        ("F3", MID, ZXY, Z2), ("D", MID, YZX, Z2), ("A3", LOW, YZX, Z3),
+    ),
+    5: (
+        ("A3", MID, ZXY, Z0),
+    ),
+    6: (
+        ("D", MID, ZXY, Z1),
+    ),
+    7: (
+        ("F2", LOW, ZXY, Z1), ("D", MID, ZXY, Z2), ("A3", LOW, XYZ), ("F3", LOW, ZXY, Z3),
+    ),
+    8: (
+        ("D", MID, YZX, Z1), ("F3", MID, YZX, Z0), ("D", MID, XYZ), ("A3", LOW, YZX, Z2), ("A3", LOW, ZXY, Z2),
+        ("F3", MID, ZXY, Z0),
+    ),
+    11: (
+        ("A3", LOW, YZX, Z1), ("F3", LOW, YZX, Z3),
+    ),
+    12: (
+        ("A3", LOW, ZXY, Z1),
+    ),
+    13: (
+        ("D", MID, ZXY, Z0), ("F3", LOW, FACTOR), ("D", MID, YZX, Z0), ("F3", LOW, XYZ),
+    ),
+    14: (
+        ("F3", LOW, ZXY, Z2), ("D", LOW, ZXY, Z3), ("F3", LOW, YZX, Z2),
+    ),
+    15: (
+        ("D", LOW, FACTOR),
+    ),
+    16: (
+        ("A3", LOW, ZXY, Z0), ("D", LOW, XYZ), ("F3", LOW, ZXY, Z1), ("F3", LOW, YZX, Z1), ("D", LOW, YZX, Z3),
+        ("A3", LOW, YZX, Z0),
+    ),
+    17: (
+        ("D", LOW, YZX, Z2), ("D", LOW, ZXY, Z2),
+    ),
+    18: (
+        ("D", LOW, YZX, Z1),
+    ),
+    19: (
+        ("F3", LOW, ZXY, Z0),
+    ),
+    20: (
+        ("D", LOW, ZXY, Z1), ("F3", LOW, YZX, Z0),
+    ),
+    22: (
+        ("D", LOW, ZXY, Z0), ("D", LOW, YZX, Z0),
+    ),
 }
 
 
@@ -174,20 +262,19 @@
     return lax.dot_general(lhs, rhs, (((1,), (0,)), ((), ())), precision=PRECISE, preferred_element_type=jnp.float32)
 
 
-def merge_factors(t, grams):
+def merge_factor(t, gram):
     row = lax.broadcasted_iota(jnp.int32, (GROUP, GROUP), 0)
     column = lax.broadcasted_iota(jnp.int32, (GROUP, GROUP), 1)
     for width in (BLK, 2 * BLK, 4 * BLK):
         above = (row // (2 * width) == column // (2 * width)) & (row // width < column // width)
-        left = [nn(t_mat, jnp.where(above, gram, 0.0)) for t_mat, gram in zip(t, grams)]
-        t = [t_mat - nn(half, t_mat) for t_mat, half in zip(t, left)]
+        t = t - nn(nn(t, jnp.where(above, gram, 0.0)), t)
     return t
 
 
 def kernel(
     z_ref, v_ref, octet_ref, t_ref, out_ref, buf, factors, acc, peer, t_buf, rows_buf, gram, gram_peer, gram_pair,
     gram_parts, gram_full,
-    send_sems, recv_sems, own_sems, z_sems, peer_send, peer_recv, octet_send, octet_recv, pair_send, pair_recv,
+    send_sems, recv_sems, own_sems, z_keep_sems, z_send_sems, z_recv_sems, peer_send, peer_recv, octet_send, octet_recv, pair_send, pair_recv,
 ):
     gather = Gather(buf, factors, send_sems, recv_sems)
     me, core = gather.me, gather.core
@@ -212,17 +299,41 @@
             device_id=partner, device_id_type=MESH,
         )
 
-    own = [
-        pltpu.make_async_copy(v_ref, buf.at[:, me["z"], me["y"], me["x"]], own_sems.at[0]),
-        pltpu.make_async_copy(octet_ref.at[:, seat], rows_buf.at[:, seat], own_sems.at[1]),
-    ]
+    own = []
     for rnd in range(ROUNDS):
-        own.append(pltpu.make_async_copy(t_ref.at[8 * rnd + col // OCTET], t_buf.at[rnd], own_sems.at[2 + rnd]))
+        chunks = pl.ds(ROUND_BASE[rnd], CHUNKS - OCTET * rnd)
+        rows = pl.ds(ROWS_BASE[rnd], ROUNDS - rnd)
+        to_buf = (v_ref.at[rnd, pl.ds(OCTET * rnd, CHUNKS - OCTET * rnd)], buf.at[chunks, me["z"], me["y"], me["x"]])
+        to_rows = (octet_ref.at[rnd, pl.ds(rnd, ROUNDS - rnd), seat], rows_buf.at[rows, seat])
+        own.append(pltpu.make_async_copy(*to_buf, own_sems.at[rnd]))
+        own.append(pltpu.make_async_copy(*to_rows, own_sems.at[ROUNDS + rnd]))
+    for rnd in range(ROUNDS):
+        own.append(pltpu.make_async_copy(t_ref.at[8 * rnd + col // OCTET], t_buf.at[rnd], own_sems.at[2 * ROUNDS + rnd]))
     for copy in own:
         copy.start()
     mine = pl.ds(core * (COLS // 2), COLS // 2)
-    z_keep = pltpu.make_async_copy(z_ref.at[core], out_ref.at[:, mine, :], z_sems.at[0])
-    z_keep.start()
+
+    def z_chunk(half, chunk):
+        return z_ref.at[:, pl.ds(pl.multiple_of((half * CHUNKS + chunk) * LANES, LANES), LANES)]
+
+    def z_keep(chunk):
+        return pltpu.make_async_copy(z_chunk(core, chunk), out_ref.at[chunk, mine], z_keep_sems.at[chunk])
+
+    def z_give(chunk):
+        return pltpu.make_async_remote_copy(
+            src_ref=z_chunk(1 - core, chunk), dst_ref=out_ref.at[chunk, mine],
+            send_sem=z_send_sems.at[chunk], recv_sem=z_recv_sems.at[chunk],
+            device_id=partner, device_id_type=MESH,
+        )
+
+    def each_chunk(action):
+        def body(chunk, _):
+            action(chunk)
+            return 0
+
+        lax.fori_loop(0, CHUNKS, body, 0)
+
+    each_chunk(lambda chunk: z_keep(chunk).start())
 
     barrier = pltpu.get_barrier_semaphore()
     peers = [gather.neighbour(axis, offset) for axis in "xyz" for offset in (1, -1)]
@@ -231,21 +342,26 @@
         pl.semaphore_signal(barrier, inc=1, device_id=device, device_id_type=MESH)
     pl.semaphore_wait(barrier, len(peers))
 
+    halves = [to_partner(2 + rnd, factors.at[core, rnd], factors.at[core, rnd]) for rnd in range(ROUNDS)]
+
     def run(events):
         for event in events:
             gather.event(*event)
-
-    spread = [to_mate(0, hop, octet_ref.at[:, at], rows_buf.at[:, seat]) for hop, at in mates.items()]
+            if event[0] == "D" and event[2] == FACTOR:
+                halves[event[1]].start()
+
+    spread = [
+        to_mate(
+            rnd, hop, octet_ref.at[rnd, pl.ds(rnd, ROUNDS - rnd), at], rows_buf.at[pl.ds(ROWS_BASE[rnd], ROUNDS - rnd), seat]
+        )
+        for rnd in range(ROUNDS) for hop, at in mates.items()
+    ]
     for copy in spread:
         copy.start()
     for copy in own:
         copy.wait()
-    run(AFTER_SPREAD)
-    z_give = pltpu.make_async_remote_copy(
-        src_ref=z_ref.at[1 - core], dst_ref=out_ref.at[:, mine, :], send_sem=z_sems.at[1], recv_sem=z_sems.at[2],
-        device_id=partner, device_id_type=MESH,
-    )
-    z_give.start()
+    run(OPENING[0])
+    each_chunk(lambda chunk: z_give(chunk).start())
     for copy in spread:
         copy.wait()
     for rnd, chunks in enumerate(((0, 1, 2), (3, 4), (5,))):
@@ -253,57 +369,63 @@
         gram[:, :, rnd] = nt(panel, panel).reshape(OCTET, 2, SHARE, GROUP)
     pair = to_partner(0, gram.at[:, 1 - core], gram_peer)
     pair.start()
-    run(AFTER_GRAM)
+    run(OPENING[1])
     pair.wait()
     gram_pair[...] = gram[:, core] + gram_peer[...]
-    scatter = [to_mate(1, hop, gram_pair.at[at], gram_parts.at[seat]) for hop, at in mates.items()]
+    scatter = [to_mate(ROUNDS, hop, gram_pair.at[at], gram_parts.at[seat]) for hop, at in mates.items()]
     for copy in scatter:
         copy.start()
     gram_parts[seat] = gram_pair[seat]
-    run(AFTER_PAIR)
+    run(OPENING[2])
     for copy in scatter:
         copy.wait()
     gram_full[core, seat] = jnp.sum(gram_parts[...], axis=0)
-    collect = [to_mate(2, hop, gram_full.at[core, seat], gram_full.at[core, seat]) for hop in mates]
+    collect = [to_mate(ROUNDS + 1, hop, gram_full.at[core, seat], gram_full.at[core, seat]) for hop in mates]
     for copy in collect:
         copy.start()
-    run(AFTER_SUM)
+    run(OPENING[3])
     for copy in collect:
         copy.wait()
     pair = to_partner(1, gram_full.at[core], gram_full.at[core])
     pair.start()
-    run(AFTER_GRAMS)
+    run(OPENING[4])
     pair.wait()
 
-    row = lax.broadcasted_iota(jnp.int32, (GROUP, GROUP), 0)
-    column = lax.broadcasted_iota(jnp.int32, (GROUP, GROUP), 1)
-    blocks = [
-        jnp.where(row // BLK == column // BLK, jnp.concatenate([t_buf[rnd]] * OCTET, axis=1), 0.0)
-        for rnd in range(ROUNDS)
-    ]
-    grams = [
-        jnp.concatenate([gram_full[half, at, rnd] for at in range(OCTET) for half in range(2)], axis=0)
-        for rnd in range(ROUNDS)
-    ]
-    for rnd, t_mat in enumerate(merge_factors(blocks, grams)):
+    def merge(rnd, _):
+        row = lax.broadcasted_iota(jnp.int32, (GROUP, GROUP), 0)
+        column = lax.broadcasted_iota(jnp.int32, (GROUP, GROUP), 1)
+        diagonal = jnp.where(row // BLK == column // BLK, jnp.concatenate([t_buf[rnd]] * OCTET, axis=1), 0.0)
+        pieces = [gram_full[half, at, rnd] for at in range(OCTET) for half in range(2)]
+        t_mat = merge_factor(diagonal, jnp.concatenate(pieces, axis=0))
         for half in range(2):
             rows_buf[2 * rnd + half] = t_mat[:, half * LANES : (half + 1) * LANES].reshape(OCTET, BLK, LANES)
         factors[core, rnd, me["z"], me["y"], me["x"]] = rows_buf[2 * rnd + core, seat]
-    run(AFTER_FACTORS)
-    halves = [to_partner(2 + rnd, factors.at[core, rnd], factors.at[core, rnd]) for rnd in range(ROUNDS)]
-    for copy in reversed(halves):
-        copy.start()
-    z_keep.wait()
-    z_give.wait()
-    for copy in halves:
-        copy.wait()
+        return 0
+
+    lax.fori_loop(0, ROUNDS, merge, 0)
+    run(OPENING[5])
+    each_chunk(lambda chunk: z_keep(chunk).wait())
+    each_chunk(lambda chunk: z_give(chunk).wait())
+
+    def over_tiles(first, body):
+        count = CHUNKS // 2 - first
+        pl.when(count % 2 == 1)(lambda: body(first, 1))
+        pl.when(count % 4 >= 2)(lambda: body(first + count % 2, 2))
+
+        def four(i, _):
+            body(first + count % 4 + 4 * i, 4)
+            return 0
+
+        lax.fori_loop(0, count // 4, four, 0)
 
     def step(idx, _):
         for at, events in BEFORE_STEP.items():
             @pl.when(idx == at)
             def _(events=events):
-                for event in events:
-                    gather.event(*event)
+                run(events)
+
+        for needed in range(ROUNDS):
+            pl.when(idx == 16 - 8 * needed)(lambda needed=needed: halves[needed].wait())
 
         group = STEPS - 1 - idx
         rnd = group // 8
@@ -324,11 +446,11 @@
 
         acc[...] = jnp.zeros_like(acc)
 
-        def project(w, _):
-            acc[...] += nt(z_tile(w), tile(w))
-            return 0
-
-        lax.fori_loop(first, CHUNKS // 2, project, 0)
+        def project(w, count):
+            z = jnp.concatenate([z_tile(w + i) for i in range(count)], axis=1)
+            acc[...] += nt(z, jnp.concatenate([tile(w + i) for i in range(count)], axis=1))
+
+        over_tiles(first, project)
 
         exchange = pltpu.make_async_remote_copy(
             src_ref=acc, dst_ref=peer.at[slot], send_sem=peer_send.at[slot], recv_sem=peer_recv.at[slot],
@@ -342,13 +464,12 @@
         exchange.wait()
         w_full = nt(acc[...] + peer[slot], t_mat)
 
-        def update(w, _):
-            delta = nn(w_full, tile(w))
-            out_ref[2 * w] -= delta[:, :LANES]
-            out_ref[2 * w + 1] -= delta[:, LANES:]
-            return 0
-
-        lax.fori_loop(first, CHUNKS // 2, update, 0)
+        def update(w, count):
+            delta = nn(w_full, jnp.concatenate([tile(w + i) for i in range(count)], axis=1))
+            for i in range(2 * count):
+                out_ref[2 * w + i] -= delta[:, i * LANES : (i + 1) * LANES]
+
+        over_tiles(first, update)
         return 0
 
     lax.fori_loop(0, STEPS, step, 0)
@@ -378,25 +499,26 @@
             vmem(2, OCTET, ROUNDS, SHARE, GROUP),
             pltpu.SemaphoreType.DMA((len(SEMS),)),
             pltpu.SemaphoreType.DMA((len(SEMS),)),
-            pltpu.SemaphoreType.DMA((2 + ROUNDS,)),
-            pltpu.SemaphoreType.DMA((3,)),
+            pltpu.SemaphoreType.DMA((3 * ROUNDS,)),
+            pltpu.SemaphoreType.DMA((CHUNKS,)),
+            pltpu.SemaphoreType.DMA((CHUNKS,)),
+            pltpu.SemaphoreType.DMA((CHUNKS,)),
             pltpu.SemaphoreType.DMA((2,)),
             pltpu.SemaphoreType.DMA((2,)),
-            pltpu.SemaphoreType.DMA((3 * OCTET,)),
-            pltpu.SemaphoreType.DMA((3 * OCTET,)),
+            pltpu.SemaphoreType.DMA(((ROUNDS + 2) * OCTET,)),
+            pltpu.SemaphoreType.DMA(((ROUNDS + 2) * OCTET,)),
             pltpu.SemaphoreType.DMA((2 + ROUNDS,)),
             pltpu.SemaphoreType.DMA((2 + ROUNDS,)),
         ],
         compiler_params=pltpu.CompilerParams(collective_id=0, has_side_effects=True, vmem_limit_bytes=67043328),
         name="apply_panels",
-    )(z, v, v.reshape(SLOTS // OCTET, OCTET, BLK, LANES), t)
+    )(z, v, v.reshape(ROUNDS, CHUNKS // OCTET, OCTET, BLK, LANES), t)
 
 
 def solution(mesh):
     def local_run(z_cols, v_local, t_local):
-        z = z_cols.reshape(2, CHUNKS, LANES, COLS // 2).transpose(0, 1, 3, 2)
+        z = z_cols.T
         v = v_local.reshape(CHUNKS, LANES, ROUNDS, BLK).transpose(2, 0, 3, 1)
-        v = jnp.concatenate([v[rnd, 8 * rnd :] for rnd in range(ROUNDS)], axis=0)
         out = apply_panels(z, v, t_local.reshape(STEPS, GROUP, BLK))
         return out.transpose(0, 2, 1).reshape(CHUNKS * LANES, COLS)
 

time: 308 us -> 250 us (0.81)
  Pallas kernels: 298 us -> 242 us
    pallas_call x1, Pallas kernels: 298 us -> 242 us  [apply_panels(): pl.pallas_call(kernel, out_shape=jax.ShapeDtypeStruct((CHUNKS, COLS, LANE...]
where the time goes in v4:
time: 250 us
  Pallas kernels  242 us (97%)
  local copies, waits for them, and re-layouts  7.73 us (3%)
    pallas_call x1, Pallas kernels, apply_panels(): pl.pallas_call(kernel, out_shape=jax.ShapeDtypeStruct((CHUNKS, COLS, LANE...  242 us

profile of v4, /device:TPU:1, one launch (start us, length us, event | category | flops | bytes accessed | tf_op | source)
XLA Modules:
  0.0 250.2 jit_solution(5951069438916331632)
XLA Ops:
  0.0 1.5 copy.9
  1.5 0.0 copy-start
  1.5 1.2 copy.13
  2.7 0.2 copy-done
  2.9 2.8 %copy.6 = f32[192,32,32]{2,1,0:T(8,128)} copy(f32[192,32,32]{0,2,1:T(8,128)S(1)} %copy-done) | data formatting | bytes 1572864 | tf_op args[2]
  5.7 242.4 %apply_panels.1 = f32[24,64,128]{2,1,0:T(8,128)} custom-call(f32[32,6144]{1,0:T(8,128)} %bitcast.22, f32[3,24,32,128]{3,2,1,0:T(8,128)} %bitcast.18, f32[3,3,8,32,128]{4,3,2,1,0:T(8,128)} %bitcast.19, f32[24,256,32]{2,1,0:T(8,128)} %bitcast.17), custom_call_target="tpu_custom_call" | custom-call | tf_op jit(solution)/shard_map/apply_panels/pallas_call | solution.py:483
  248.1 2.1 copy_bitcast_fusion
Async XLA Ops:
  1.5 1.4 copy-start

commit v5 on v4

--- a/solution.py
+++ b/solution.py
@@ -20,8 +20,8 @@
 ORDER = (("x", "y", "z"), ("y", "z", "x"), ("z", "x", "y"))
 SHARES = {
     24: (4, 10, 10), 22: (4, 9, 9), 20: (4, 8, 8), 18: (4, 7, 7),
-    16: (6, 5, 5), 14: (4, 5, 5), 12: (4, 4, 4), 10: (4, 3, 3),
-    8: (2, 3, 3), 6: (2, 2, 2), 4: (2, 1, 1), 2: (1, 0, 1),
+    16: (4, 6, 6), 14: (4, 5, 5), 12: (4, 4, 4), 10: (4, 3, 3),
+    8: (2, 3, 3), 6: (2, 2, 2), 4: (2, 1, 1), 2: (1, 1, 0),
 }
 ROWS_BASE = (0, 3, 5)
 ROUND_BASE = (0, 24, 40)
@@ -157,96 +157,87 @@
 Z0, Z1, Z2, Z3 = range(SIDE)
 OPENING = (
     (
-        ("A1", TOP, ZXY), ("A1", TOP, YZX), ("A1", TOP, XYZ), ("A1", LOW, XYZ), ("A1", MID, XYZ), ("A1", LOW, ZXY),
-        ("A1", MID, YZX), ("F1", TOP, YZX), ("F1", TOP, ZXY), ("A1", LOW, YZX), ("A1", MID, ZXY), ("F1", MID, YZX),
-        ("F1", LOW, XYZ), ("F1", LOW, ZXY), ("F1", TOP, XYZ), ("A2", TOP, ZXY, Z3), ("A2", TOP, YZX),
-        ("A2", TOP, ZXY, Z2), ("A2", TOP, ZXY, Z0), ("F1", MID, XYZ), ("A2", TOP, ZXY, Z1),
+        ("A1", TOP, ZXY), ("A1", TOP, YZX), ("A1", TOP, XYZ), ("A1", MID, ZXY), ("A1", LOW, XYZ), ("A1", LOW, ZXY),
+        ("A1", MID, YZX), ("A1", MID, XYZ), ("F1", TOP, YZX), ("F1", TOP, ZXY), ("A1", LOW, YZX),
     ),
     (
-        ("F2", TOP, ZXY, Z3), ("A2", LOW, ZXY, Z3), ("A2", TOP, XYZ), ("A2", MID, YZX), ("F1", LOW, YZX),
-        ("A2", LOW, ZXY, Z1), ("F2", TOP, YZX),
+        ("F1", MID, ZXY), ("F1", MID, XYZ), ("A2", TOP, YZX), ("A2", TOP, ZXY, Z3), ("A2", MID, ZXY, Z3),
+        ("A2", TOP, ZXY, Z0), ("F1", LOW, ZXY), ("F1", MID, YZX), ("A2", TOP, ZXY, Z2), ("A2", MID, ZXY, Z1),
     ),
     (
-        ("A2", MID, XYZ), ("F2", TOP, ZXY, Z1), ("F2", LOW, ZXY, Z3), ("F1", MID, ZXY), ("A2", LOW, ZXY, Z2),
-        ("A2", LOW, YZX),
+        ("F1", LOW, YZX), ("A2", TOP, ZXY, Z1), ("F2", MID, ZXY, Z3), ("A2", MID, XYZ), ("F2", TOP, YZX),
+        ("A2", MID, YZX),
     ),
     (
-        ("F2", TOP, XYZ), ("A3", TOP, ZXY, Z3),
+        ("F2", TOP, ZXY, Z0), ("F2", TOP, ZXY, Z3), ("F1", TOP, XYZ), ("F2", TOP, ZXY, Z2), ("A2", LOW, ZXY, Z3),
+        ("A3", MID, ZXY, Z3),
     ),
     (
-        ("A3", TOP, YZX, Z3), ("A3", LOW, ZXY, Z3), ("A2", LOW, ZXY, Z0), ("A3", TOP, YZX, Z2), ("A2", MID, ZXY, Z3),
-        ("A2", MID, ZXY, Z0), ("A3", TOP, YZX, Z0), ("A2", MID, ZXY, Z2), ("F2", MID, YZX),
+        ("A3", TOP, ZXY, Z3), ("A2", MID, ZXY, Z2), ("A3", TOP, YZX, Z3), ("A2", TOP, XYZ), ("A2", LOW, ZXY, Z2),
+        ("A3", TOP, ZXY, Z0), ("A3", TOP, YZX, Z0), ("A2", LOW, YZX), ("A2", LOW, ZXY, Z1),
     ),
     (
-        ("F2", LOW, ZXY, Z0), ("A1", MID, FACTOR), ("A3", TOP, ZXY, Z1), ("A2", MID, ZXY, Z1), ("F2", TOP, ZXY, Z2),
-        ("F2", TOP, ZXY, Z0), ("A2", LOW, XYZ), ("A1", TOP, FACTOR), ("A3", TOP, XYZ), ("A3", MID, YZX, Z3),
-        ("A1", LOW, FACTOR), ("F1", TOP, FACTOR), ("A3", TOP, ZXY, Z2), ("F1", MID, FACTOR), ("A3", TOP, YZX, Z1),
-        ("F3", TOP, ZXY, Z1), ("F2", LOW, YZX), ("F3", TOP, ZXY, Z3), ("F3", TOP, YZX, Z0), ("A3", TOP, ZXY, Z0),
-        ("F2", MID, ZXY, Z3), ("A2", TOP, FACTOR), ("F3", TOP, YZX, Z2), ("F2", MID, ZXY, Z2), ("A2", MID, FACTOR),
-        ("F3", TOP, XYZ), ("F2", MID, ZXY, Z0), ("F1", LOW, FACTOR), ("F2", MID, XYZ), ("F3", MID, YZX, Z3),
-        ("F2", TOP, FACTOR), ("F3", TOP, YZX, Z3), ("A3", MID, ZXY, Z3), ("D", TOP, YZX, Z2), ("F3", TOP, YZX, Z1),
-        ("A3", MID, YZX, Z1), ("F2", MID, FACTOR), ("F3", TOP, ZXY, Z0), ("A3", MID, XYZ), ("D", TOP, XYZ),
-        ("A2", LOW, FACTOR), ("A3", TOP, FACTOR), ("F3", MID, ZXY, Z3), ("F2", MID, ZXY, Z1), ("D", TOP, ZXY, Z1),
-        ("A3", MID, YZX, Z2), ("D", TOP, YZX, Z0), ("D", MID, YZX, Z3), ("F2", LOW, FACTOR), ("A3", MID, FACTOR),
-        ("A3", MID, YZX, Z0), ("D", TOP, YZX, Z1), ("F3", TOP, FACTOR), ("F3", TOP, ZXY, Z2), ("A3", MID, ZXY, Z1),
-        ("F3", MID, FACTOR), ("F3", MID, YZX, Z2), ("D", TOP, ZXY, Z3), ("F2", LOW, XYZ), ("D", TOP, YZX, Z3),
-        ("D", TOP, FACTOR), ("D", TOP, ZXY, Z0), ("A3", MID, ZXY, Z2), ("F3", MID, ZXY, Z1), ("F2", LOW, ZXY, Z2),
-        ("A3", LOW, FACTOR), ("D", TOP, ZXY, Z2),
+        ("A1", TOP, FACTOR), ("F2", LOW, ZXY, Z3), ("A3", TOP, ZXY, Z2), ("F2", MID, YZX), ("A1", MID, FACTOR),
+        ("F2", MID, ZXY, Z2), ("F2", MID, XYZ), ("F3", TOP, ZXY, Z3), ("F1", LOW, XYZ), ("A2", MID, ZXY, Z0),
+        ("F2", MID, ZXY, Z1), ("A3", TOP, YZX, Z1), ("F1", MID, FACTOR), ("F2", TOP, XYZ), ("F3", TOP, YZX, Z0),
+        ("F3", MID, ZXY, Z3), ("A2", MID, FACTOR), ("F3", TOP, YZX, Z3), ("A1", LOW, FACTOR), ("F3", TOP, ZXY, Z0),
+        ("A3", TOP, YZX, Z2), ("F1", TOP, FACTOR), ("F2", TOP, ZXY, Z1), ("A3", MID, ZXY, Z2), ("A3", TOP, XYZ),
+        ("A3", MID, YZX, Z3), ("F2", MID, FACTOR), ("F3", TOP, ZXY, Z2), ("F1", LOW, FACTOR), ("A3", LOW, ZXY, Z3),
+        ("A2", TOP, FACTOR), ("A3", MID, YZX, Z2), ("F3", TOP, XYZ), ("A3", MID, XYZ), ("F2", TOP, FACTOR),
+        ("D", TOP, ZXY, Z2), ("A3", MID, YZX, Z1), ("D", TOP, YZX, Z3), ("F3", TOP, YZX, Z2), ("F3", TOP, YZX, Z1),
+        ("D", MID, ZXY, Z3), ("A3", TOP, ZXY, Z1), ("A3", TOP, FACTOR), ("D", TOP, XYZ), ("F2", LOW, YZX),
+        ("A3", MID, FACTOR), ("F3", TOP, ZXY, Z1), ("F3", MID, YZX, Z1), ("D", TOP, ZXY, Z3), ("F3", TOP, FACTOR),
+        ("A2", LOW, FACTOR), ("D", TOP, YZX, Z2), ("F3", MID, YZX, Z3), ("D", TOP, FACTOR), ("A2", LOW, XYZ),
+        ("D", TOP, ZXY, Z1), ("F2", LOW, ZXY, Z1), ("D", TOP, YZX, Z0), ("F3", MID, YZX, Z2), ("A3", MID, ZXY, Z1),
+        ("D", TOP, YZX, Z1), ("A3", MID, YZX, Z0), ("D", TOP, ZXY, Z0),
     ),
 )
 BEFORE_STEP = {
-    1: (
-        ("F3", MID, XYZ), ("D", MID, ZXY, Z3),
-    ),
     3: (
-        ("F3", MID, YZX, Z1), ("D", MID, FACTOR),
+        ("F3", MID, FACTOR), ("F2", MID, ZXY, Z0),
     ),
     4: (
-        ("F3", MID, ZXY, Z2), ("D", MID, YZX, Z2), ("A3", LOW, YZX, Z3),
+        ("F2", LOW, FACTOR), ("F3", LOW, ZXY, Z3),
     ),
     5: (
-        ("A3", MID, ZXY, Z0),
+        ("F3", MID, ZXY, Z1), ("F3", MID, ZXY, Z2), ("F2", LOW, ZXY, Z2), ("D", MID, YZX, Z2), ("F3", MID, XYZ),
+        ("F2", LOW, XYZ),
     ),
     6: (
-        ("D", MID, ZXY, Z1),
+        ("D", MID, FACTOR), ("D", MID, YZX, Z3), ("F3", MID, YZX, Z0), ("A3", LOW, YZX, Z3), ("A3", LOW, FACTOR),
+        ("D", MID, YZX, Z1),
     ),
     7: (
-        ("F2", LOW, ZXY, Z1), ("D", MID, ZXY, Z2), ("A3", LOW, XYZ), ("F3", LOW, ZXY, Z3),
+        ("A3", MID, ZXY, Z0), ("D", MID, ZXY, Z1),
     ),
     8: (
-        ("D", MID, YZX, Z1), ("F3", MID, YZX, Z0), ("D", MID, XYZ), ("A3", LOW, YZX, Z2), ("A3", LOW, ZXY, Z2),
-        ("F3", MID, ZXY, Z0),
+        ("D", MID, YZX, Z0), ("D", MID, ZXY, Z2), ("A3", LOW, YZX, Z2), ("A2", LOW, ZXY, Z0), ("D", LOW, ZXY, Z3),
+        ("A3", LOW, ZXY, Z2), ("A3", LOW, XYZ), ("D", MID, XYZ),
     ),
     11: (
-        ("A3", LOW, YZX, Z1), ("F3", LOW, YZX, Z3),
+        ("F3", MID, ZXY, Z0), ("A3", LOW, ZXY, Z1), ("A3", LOW, YZX, Z1),
     ),
     12: (
-        ("A3", LOW, ZXY, Z1),
-    ),
-    13: (
-        ("D", MID, ZXY, Z0), ("F3", LOW, FACTOR), ("D", MID, YZX, Z0), ("F3", LOW, XYZ),
+        ("F3", LOW, FACTOR),
     ),
     14: (
-        ("F3", LOW, ZXY, Z2), ("D", LOW, ZXY, Z3), ("F3", LOW, YZX, Z2),
+        ("F3", LOW, XYZ), ("F3", LOW, ZXY, Z2), ("F3", LOW, YZX, Z3), ("D", MID, ZXY, Z0), ("F2", LOW, ZXY, Z0),
     ),
     15: (
-        ("D", LOW, FACTOR),
+        ("F3", LOW, YZX, Z2), ("F3", LOW, ZXY, Z1), ("D", LOW, FACTOR),
     ),
     16: (
-        ("A3", LOW, ZXY, Z0), ("D", LOW, XYZ), ("F3", LOW, ZXY, Z1), ("F3", LOW, YZX, Z1), ("D", LOW, YZX, Z3),
-        ("A3", LOW, YZX, Z0),
-    ),
-    17: (
-        ("D", LOW, YZX, Z2), ("D", LOW, ZXY, Z2),
+        ("A3", LOW, ZXY, Z0), ("A3", LOW, YZX, Z0), ("D", LOW, YZX, Z3), ("D", LOW, ZXY, Z2), ("F3", LOW, YZX, Z1),
+        ("D", LOW, XYZ),
     ),
     18: (
-        ("D", LOW, YZX, Z1),
+        ("D", LOW, YZX, Z2),
     ),
     19: (
         ("F3", LOW, ZXY, Z0),
     ),
     20: (
-        ("D", LOW, ZXY, Z1), ("F3", LOW, YZX, Z0),
+        ("D", LOW, YZX, Z1), ("F3", LOW, YZX, Z0), ("D", LOW, ZXY, Z1),
     ),
     22: (
         ("D", LOW, ZXY, Z0), ("D", LOW, YZX, Z0),
@@ -396,7 +387,7 @@
         column = lax.broadcasted_iota(jnp.int32, (GROUP, GROUP), 1)
         diagonal = jnp.where(row // BLK == column // BLK, jnp.concatenate([t_buf[rnd]] * OCTET, axis=1), 0.0)
         pieces = [gram_full[half, at, rnd] for at in range(OCTET) for half in range(2)]
-        t_mat = merge_factor(diagonal, jnp.concatenate(pieces, axis=0))
+        t_mat = merge_factor(diagonal, jnp.concatenate(pieces, axis=0)).T
         for half in range(2):
             rows_buf[2 * rnd + half] = t_mat[:, half * LANES : (half + 1) * LANES].reshape(OCTET, BLK, LANES)
         factors[core, rnd, me["z"], me["y"], me["x"]] = rows_buf[2 * rnd + core, seat]
@@ -462,7 +453,7 @@
             [factors[half, rnd, plane, pl.ds(pair_row, 2)].reshape(GROUP, LANES) for half in range(2)], axis=1
         )
         exchange.wait()
-        w_full = nt(acc[...] + peer[slot], t_mat)
+        w_full = nn(acc[...] + peer[slot], t_mat)
 
         def update(w, count):
             delta = nn(w_full, jnp.concatenate([tile(w + i) for i in range(count)], axis=1))

time: 250 us -> 238 us (0.952)
  Pallas kernels: 242 us -> 230 us
    pallas_call x1, Pallas kernels: 242 us -> 230 us  [apply_panels(): pl.pallas_call(kernel, out_shape=jax.ShapeDtypeStruct((CHUNKS, COLS, LANE...]
where the time goes in v5:
time: 238 us
  Pallas kernels  230 us (97%)
  local copies, waits for them, and re-layouts  7.73 us (3%)
    pallas_call x1, Pallas kernels, apply_panels(): pl.pallas_call(kernel, out_shape=jax.ShapeDtypeStruct((CHUNKS, COLS, LANE...  230 us

profile of v5, /device:TPU:1, one launch (start us, length us, event | category | flops | bytes accessed | tf_op | source)
XLA Modules:
  0.0 238.2 jit_solution(12585686535019529170)
XLA Ops:
  0.0 1.5 copy.9
  1.5 0.0 copy-start
  1.5 1.2 copy.13
  2.7 0.2 copy-done
  2.9 2.8 %copy.6 = f32[192,32,32]{2,1,0:T(8,128)} copy(f32[192,32,32]{0,2,1:T(8,128)S(1)} %copy-done) | data formatting | bytes 1572864 | tf_op args[2]
  5.7 230.5 %apply_panels.1 = f32[24,64,128]{2,1,0:T(8,128)} custom-call(f32[32,6144]{1,0:T(8,128)} %bitcast.22, f32[3,24,32,128]{3,2,1,0:T(8,128)} %bitcast.18, f32[3,3,8,32,128]{4,3,2,1,0:T(8,128)} %bitcast.19, f32[24,256,32]{2,1,0:T(8,128)} %bitcast.17), custom_call_target="tpu_custom_call" | custom-call | tf_op jit(solution)/shard_map/apply_panels/pallas_call | solution.py:474
  236.2 2.1 copy_bitcast_fusion
Async XLA Ops:
  1.5 1.4 copy-start

commit v6 on v5

--- a/solution.py
+++ b/solution.py
@@ -157,90 +157,84 @@
 Z0, Z1, Z2, Z3 = range(SIDE)
 OPENING = (
     (
-        ("A1", TOP, ZXY), ("A1", TOP, YZX), ("A1", TOP, XYZ), ("A1", MID, ZXY), ("A1", LOW, XYZ), ("A1", LOW, ZXY),
-        ("A1", MID, YZX), ("A1", MID, XYZ), ("F1", TOP, YZX), ("F1", TOP, ZXY), ("A1", LOW, YZX),
+        ("A1", MID, ZXY), ("A1", TOP, YZX), ("A1", TOP, XYZ), ("A1", TOP, ZXY), ("A1", MID, XYZ), ("A1", MID, YZX),
+        ("A1", LOW, ZXY), ("F1", TOP, XYZ), ("A1", LOW, XYZ), ("F1", TOP, YZX), ("F1", MID, ZXY),
     ),
     (
-        ("F1", MID, ZXY), ("F1", MID, XYZ), ("A2", TOP, YZX), ("A2", TOP, ZXY, Z3), ("A2", MID, ZXY, Z3),
-        ("A2", TOP, ZXY, Z0), ("F1", LOW, ZXY), ("F1", MID, YZX), ("A2", TOP, ZXY, Z2), ("A2", MID, ZXY, Z1),
+        ("F1", MID, XYZ), ("F1", TOP, ZXY), ("A2", TOP, YZX), ("A2", TOP, XYZ), ("F1", LOW, XYZ),
     ),
     (
-        ("F1", LOW, YZX), ("A2", TOP, ZXY, Z1), ("F2", MID, ZXY, Z3), ("A2", MID, XYZ), ("F2", TOP, YZX),
-        ("A2", MID, YZX),
+        ("A2", MID, ZXY, Z3), ("A2", MID, ZXY, Z2), ("F1", LOW, ZXY), ("A2", TOP, ZXY, Z3), ("A2", TOP, ZXY, Z0),
+        ("F1", MID, YZX), ("A2", TOP, ZXY, Z1), ("A2", MID, XYZ), ("A2", TOP, ZXY, Z2), ("F2", TOP, XYZ),
+        ("F2", TOP, YZX), ("A2", MID, ZXY, Z1), ("A2", MID, YZX), ("F2", MID, ZXY, Z3), ("A2", LOW, ZXY, Z3),
     ),
     (
-        ("F2", TOP, ZXY, Z0), ("F2", TOP, ZXY, Z3), ("F1", TOP, XYZ), ("F2", TOP, ZXY, Z2), ("A2", LOW, ZXY, Z3),
-        ("A3", MID, ZXY, Z3),
+        ("A1", LOW, YZX), ("A3", TOP, YZX, Z3), ("A2", LOW, XYZ), ("A3", MID, ZXY, Z3), ("F2", TOP, ZXY, Z0),
+        ("F2", TOP, ZXY, Z1),
     ),
     (
-        ("A3", TOP, ZXY, Z3), ("A2", MID, ZXY, Z2), ("A3", TOP, YZX, Z3), ("A2", TOP, XYZ), ("A2", LOW, ZXY, Z2),
-        ("A3", TOP, ZXY, Z0), ("A3", TOP, YZX, Z0), ("A2", LOW, YZX), ("A2", LOW, ZXY, Z1),
+        ("F2", MID, XYZ), ("A2", MID, ZXY, Z0), ("F2", TOP, ZXY, Z3), ("A3", TOP, XYZ), ("F2", TOP, ZXY, Z2),
+        ("A3", TOP, YZX, Z0), ("A2", LOW, ZXY, Z1), ("F2", MID, ZXY, Z1), ("A2", LOW, ZXY, Z0),
     ),
     (
-        ("A1", TOP, FACTOR), ("F2", LOW, ZXY, Z3), ("A3", TOP, ZXY, Z2), ("F2", MID, YZX), ("A1", MID, FACTOR),
-        ("F2", MID, ZXY, Z2), ("F2", MID, XYZ), ("F3", TOP, ZXY, Z3), ("F1", LOW, XYZ), ("A2", MID, ZXY, Z0),
-        ("F2", MID, ZXY, Z1), ("A3", TOP, YZX, Z1), ("F1", MID, FACTOR), ("F2", TOP, XYZ), ("F3", TOP, YZX, Z0),
-        ("F3", MID, ZXY, Z3), ("A2", MID, FACTOR), ("F3", TOP, YZX, Z3), ("A1", LOW, FACTOR), ("F3", TOP, ZXY, Z0),
-        ("A3", TOP, YZX, Z2), ("F1", TOP, FACTOR), ("F2", TOP, ZXY, Z1), ("A3", MID, ZXY, Z2), ("A3", TOP, XYZ),
-        ("A3", MID, YZX, Z3), ("F2", MID, FACTOR), ("F3", TOP, ZXY, Z2), ("F1", LOW, FACTOR), ("A3", LOW, ZXY, Z3),
-        ("A2", TOP, FACTOR), ("A3", MID, YZX, Z2), ("F3", TOP, XYZ), ("A3", MID, XYZ), ("F2", TOP, FACTOR),
-        ("D", TOP, ZXY, Z2), ("A3", MID, YZX, Z1), ("D", TOP, YZX, Z3), ("F3", TOP, YZX, Z2), ("F3", TOP, YZX, Z1),
-        ("D", MID, ZXY, Z3), ("A3", TOP, ZXY, Z1), ("A3", TOP, FACTOR), ("D", TOP, XYZ), ("F2", LOW, YZX),
-        ("A3", MID, FACTOR), ("F3", TOP, ZXY, Z1), ("F3", MID, YZX, Z1), ("D", TOP, ZXY, Z3), ("F3", TOP, FACTOR),
-        ("A2", LOW, FACTOR), ("D", TOP, YZX, Z2), ("F3", MID, YZX, Z3), ("D", TOP, FACTOR), ("A2", LOW, XYZ),
-        ("D", TOP, ZXY, Z1), ("F2", LOW, ZXY, Z1), ("D", TOP, YZX, Z0), ("F3", MID, YZX, Z2), ("A3", MID, ZXY, Z1),
-        ("D", TOP, YZX, Z1), ("A3", MID, YZX, Z0), ("D", TOP, ZXY, Z0),
+        ("F2", LOW, ZXY, Z3), ("A3", TOP, ZXY, Z3), ("F3", TOP, YZX, Z0), ("F2", MID, ZXY, Z0), ("A3", TOP, YZX, Z1),
+        ("A1", MID, FACTOR), ("F3", MID, ZXY, Z3), ("A1", TOP, FACTOR), ("F2", MID, YZX), ("A3", TOP, YZX, Z2),
+        ("F1", TOP, FACTOR), ("F1", LOW, YZX), ("F1", MID, FACTOR), ("F3", TOP, ZXY, Z3), ("F3", TOP, XYZ),
+        ("A3", TOP, ZXY, Z2), ("A3", TOP, ZXY, Z1), ("A3", LOW, ZXY, Z3), ("A1", LOW, FACTOR), ("A2", TOP, FACTOR),
+        ("F2", MID, ZXY, Z2), ("A2", MID, FACTOR), ("A3", MID, YZX, Z3), ("A2", LOW, YZX), ("F3", TOP, YZX, Z3),
+        ("F1", LOW, FACTOR), ("A3", TOP, ZXY, Z0), ("A2", LOW, ZXY, Z2), ("D", TOP, ZXY, Z3), ("F2", MID, FACTOR),
+        ("D", TOP, YZX, Z0), ("D", TOP, XYZ), ("F2", TOP, FACTOR), ("D", TOP, YZX, Z3), ("F3", TOP, YZX, Z2),
+        ("A3", MID, YZX, Z1), ("A3", TOP, FACTOR), ("D", MID, ZXY, Z3), ("A2", LOW, FACTOR), ("A3", MID, XYZ),
+        ("F2", LOW, ZXY, Z0), ("F3", TOP, YZX, Z1), ("F3", TOP, ZXY, Z1), ("F3", MID, YZX, Z1), ("F3", TOP, FACTOR),
+        ("F3", TOP, ZXY, Z0), ("F3", TOP, ZXY, Z2), ("F2", LOW, XYZ), ("F2", LOW, FACTOR), ("D", TOP, YZX, Z2),
+        ("A3", MID, ZXY, Z2), ("F2", LOW, ZXY, Z2), ("A3", MID, FACTOR), ("D", TOP, FACTOR), ("D", TOP, ZXY, Z1),
     ),
 )
 BEFORE_STEP = {
-    3: (
-        ("F3", MID, FACTOR), ("F2", MID, ZXY, Z0),
+    1: (
+        ("F2", LOW, YZX), ("A3", MID, YZX, Z2), ("D", TOP, ZXY, Z2), ("F3", MID, FACTOR), ("A3", MID, ZXY, Z1),
+        ("A3", MID, ZXY, Z0), ("D", TOP, YZX, Z1), ("A3", MID, YZX, Z0),
     ),
     4: (
-        ("F2", LOW, FACTOR), ("F3", LOW, ZXY, Z3),
+        ("F3", MID, XYZ),
     ),
     5: (
-        ("F3", MID, ZXY, Z1), ("F3", MID, ZXY, Z2), ("F2", LOW, ZXY, Z2), ("D", MID, YZX, Z2), ("F3", MID, XYZ),
-        ("F2", LOW, XYZ),
+        ("F3", MID, YZX, Z3), ("A3", LOW, FACTOR), ("A3", LOW, XYZ), ("D", TOP, ZXY, Z0), ("F3", MID, ZXY, Z2),
     ),
     6: (
-        ("D", MID, FACTOR), ("D", MID, YZX, Z3), ("F3", MID, YZX, Z0), ("A3", LOW, YZX, Z3), ("A3", LOW, FACTOR),
-        ("D", MID, YZX, Z1),
-    ),
-    7: (
-        ("A3", MID, ZXY, Z0), ("D", MID, ZXY, Z1),
+        ("A3", LOW, ZXY, Z2), ("F3", MID, YZX, Z2), ("A3", LOW, YZX, Z3), ("D", MID, FACTOR), ("F3", MID, ZXY, Z1),
     ),
     8: (
-        ("D", MID, YZX, Z0), ("D", MID, ZXY, Z2), ("A3", LOW, YZX, Z2), ("A2", LOW, ZXY, Z0), ("D", LOW, ZXY, Z3),
-        ("A3", LOW, ZXY, Z2), ("A3", LOW, XYZ), ("D", MID, XYZ),
+        ("D", MID, YZX, Z3), ("A3", LOW, YZX, Z2), ("F3", MID, YZX, Z0), ("F3", LOW, ZXY, Z3), ("D", MID, YZX, Z2),
+        ("D", MID, ZXY, Z2), ("D", MID, YZX, Z1), ("F3", MID, ZXY, Z0), ("F2", LOW, ZXY, Z1), ("D", MID, XYZ),
     ),
     11: (
-        ("F3", MID, ZXY, Z0), ("A3", LOW, ZXY, Z1), ("A3", LOW, YZX, Z1),
+        ("F3", LOW, YZX, Z3),
     ),
     12: (
-        ("F3", LOW, FACTOR),
+        ("F3", LOW, FACTOR), ("D", MID, ZXY, Z1),
+    ),
+    13: (
+        ("F3", LOW, ZXY, Z2), ("F3", LOW, YZX, Z2),
     ),
     14: (
-        ("F3", LOW, XYZ), ("F3", LOW, ZXY, Z2), ("F3", LOW, YZX, Z3), ("D", MID, ZXY, Z0), ("F2", LOW, ZXY, Z0),
+        ("F3", LOW, XYZ), ("D", MID, ZXY, Z0), ("D", MID, YZX, Z0), ("A3", LOW, YZX, Z1), ("D", LOW, ZXY, Z3),
+        ("A3", LOW, ZXY, Z1), ("A3", LOW, YZX, Z0), ("A3", LOW, ZXY, Z0),
     ),
     15: (
-        ("F3", LOW, YZX, Z2), ("F3", LOW, ZXY, Z1), ("D", LOW, FACTOR),
+        ("D", LOW, FACTOR), ("D", LOW, ZXY, Z2), ("D", LOW, YZX, Z2),
     ),
     16: (
-        ("A3", LOW, ZXY, Z0), ("A3", LOW, YZX, Z0), ("D", LOW, YZX, Z3), ("D", LOW, ZXY, Z2), ("F3", LOW, YZX, Z1),
-        ("D", LOW, XYZ),
-    ),
-    18: (
-        ("D", LOW, YZX, Z2),
-    ),
-    19: (
-        ("F3", LOW, ZXY, Z0),
+        ("D", LOW, YZX, Z3), ("D", LOW, XYZ),
+    ),
+    17: (
+        ("F3", LOW, ZXY, Z1), ("F3", LOW, YZX, Z1),
     ),
     20: (
-        ("D", LOW, YZX, Z1), ("F3", LOW, YZX, Z0), ("D", LOW, ZXY, Z1),
+        ("F3", LOW, ZXY, Z0), ("D", LOW, ZXY, Z1), ("D", LOW, YZX, Z1), ("F3", LOW, YZX, Z0),
     ),
     22: (
-        ("D", LOW, ZXY, Z0), ("D", LOW, YZX, Z0),
+        ("D", LOW, YZX, Z0), ("D", LOW, ZXY, Z0),
     ),
 }
 
@@ -258,7 +252,9 @@
     column = lax.broadcasted_iota(jnp.int32, (GROUP, GROUP), 1)
     for width in (BLK, 2 * BLK, 4 * BLK):
         above = (row // (2 * width) == column // (2 * width)) & (row // width < column // width)
-        t = t - nn(nn(t, jnp.where(above, gram, 0.0)), t)
+        upper, lower = (t.reshape(-1, 2, width, GROUP)[:, half].reshape(GROUP // 2, GROUP) for half in range(2))
+        upper = upper - nn(nn(upper, jnp.where(above, gram, 0.0)), t)
+        t = jnp.stack([half.reshape(-1, width, GROUP) for half in (upper, lower)], axis=1).reshape(GROUP, GROUP)
     return t
 
 
@@ -400,14 +396,10 @@
 
     def over_tiles(first, body):
         count = CHUNKS // 2 - first
-        pl.when(count % 2 == 1)(lambda: body(first, 1))
-        pl.when(count % 4 >= 2)(lambda: body(first + count % 2, 2))
-
-        def four(i, _):
-            body(first + count % 4 + 4 * i, 4)
-            return 0
-
-        lax.fori_loop(0, count // 4, four, 0)
+        for size in (1, 2):
+            pl.when(count // size % 2 == 1)(lambda size=size: body(first + count % size, size))
+        for fours in (1, 2, 3):
+            pl.when(count // 4 == fours)(lambda fours=fours: body(first + count % 4, 4 * fours))
 
     def step(idx, _):
         for at, events in BEFORE_STEP.items():

time: 238 us -> 236 us (level)
    pallas_call x1, Pallas kernels: 230 us -> 228 us  [apply_panels(): pl.pallas_call(kernel, out_shape=jax.ShapeDtypeStruct((CHUNKS, COLS, LANE...]
where the time goes in v6:
time: 236 us
  Pallas kernels  228 us (97%)
  local copies, waits for them, and re-layouts  7.73 us (3%)
    pallas_call x1, Pallas kernels, apply_panels(): pl.pallas_call(kernel, out_shape=jax.ShapeDtypeStruct((CHUNKS, COLS, LANE...  228 us

profile of v6, /device:TPU:1, one launch (start us, length us, event | category | flops | bytes accessed | tf_op | source)
XLA Modules:
  0.0 235.8 jit_solution(6674015167373626024)
XLA Ops:
  0.0 1.5 copy.9
  1.5 0.0 copy-start
  1.5 1.2 copy.13
  2.7 0.2 copy-done
  2.9 2.8 %copy.6 = f32[192,32,32]{2,1,0:T(8,128)} copy(f32[192,32,32]{0,2,1:T(8,128)S(1)} %copy-done) | data formatting | bytes 1572864 | tf_op args[2]
  5.7 228.0 %apply_panels.1 = f32[24,64,128]{2,1,0:T(8,128)} custom-call(f32[32,6144]{1,0:T(8,128)} %bitcast.22, f32[3,24,32,128]{3,2,1,0:T(8,128)} %bitcast.18, f32[3,3,8,32,128]{4,3,2,1,0:T(8,128)} %bitcast.19, f32[24,256,32]{2,1,0:T(8,128)} %bitcast.17), custom_call_target="tpu_custom_call" | custom-call | tf_op jit(solution)/shard_map/apply_panels/pallas_call | solution.py:466
  233.7 2.1 copy_bitcast_fusion
Async XLA Ops:
  1.5 1.4 copy-start

commit v7 on v6

--- a/solution.py
+++ b/solution.py
@@ -157,84 +157,98 @@
 Z0, Z1, Z2, Z3 = range(SIDE)
 OPENING = (
     (
-        ("A1", MID, ZXY), ("A1", TOP, YZX), ("A1", TOP, XYZ), ("A1", TOP, ZXY), ("A1", MID, XYZ), ("A1", MID, YZX),
-        ("A1", LOW, ZXY), ("F1", TOP, XYZ), ("A1", LOW, XYZ), ("F1", TOP, YZX), ("F1", MID, ZXY),
+        ("A1", TOP, ZXY), ("A1", TOP, YZX), ("A1", LOW, ZXY), ("A1", MID, YZX), ("A1", TOP, XYZ), ("A1", LOW, XYZ),
+        ("F1", TOP, ZXY), ("A1", MID, XYZ), ("A1", MID, ZXY), ("F1", TOP, YZX), ("F1", TOP, XYZ),
     ),
     (
-        ("F1", MID, XYZ), ("F1", TOP, ZXY), ("A2", TOP, YZX), ("A2", TOP, XYZ), ("F1", LOW, XYZ),
+        ("F1", LOW, ZXY), ("F1", MID, YZX), ("A2", TOP, ZXY, Z3), ("A2", TOP, ZXY, Z1), ("A2", TOP, XYZ),
+        ("A2", TOP, ZXY, Z0), ("A2", TOP, ZXY, Z2), ("A2", TOP, YZX), ("F1", MID, ZXY), ("F1", MID, XYZ),
+        ("A2", LOW, ZXY, Z3),
     ),
     (
-        ("A2", MID, ZXY, Z3), ("A2", MID, ZXY, Z2), ("F1", LOW, ZXY), ("A2", TOP, ZXY, Z3), ("A2", TOP, ZXY, Z0),
-        ("F1", MID, YZX), ("A2", TOP, ZXY, Z1), ("A2", MID, XYZ), ("A2", TOP, ZXY, Z2), ("F2", TOP, XYZ),
-        ("F2", TOP, YZX), ("A2", MID, ZXY, Z1), ("A2", MID, YZX), ("F2", MID, ZXY, Z3), ("A2", LOW, ZXY, Z3),
+        ("A1", LOW, YZX), ("F2", TOP, ZXY, Z3), ("A2", LOW, ZXY, Z0), ("F2", TOP, YZX),
     ),
     (
-        ("A1", LOW, YZX), ("A3", TOP, YZX, Z3), ("A2", LOW, XYZ), ("A3", MID, ZXY, Z3), ("F2", TOP, ZXY, Z0),
-        ("F2", TOP, ZXY, Z1),
+        ("A2", MID, YZX), ("F1", LOW, XYZ), ("F2", TOP, XYZ), ("A2", MID, XYZ), ("A2", MID, ZXY, Z3),
+        ("F1", LOW, YZX), ("F2", LOW, ZXY, Z3), ("A3", TOP, YZX, Z3), ("F2", LOW, ZXY, Z0), ("A3", TOP, XYZ),
+        ("A3", TOP, ZXY, Z3),
     ),
     (
-        ("F2", MID, XYZ), ("A2", MID, ZXY, Z0), ("F2", TOP, ZXY, Z3), ("A3", TOP, XYZ), ("F2", TOP, ZXY, Z2),
-        ("A3", TOP, YZX, Z0), ("A2", LOW, ZXY, Z1), ("F2", MID, ZXY, Z1), ("A2", LOW, ZXY, Z0),
+        ("A3", TOP, YZX, Z1), ("A2", MID, ZXY, Z1), ("F2", TOP, ZXY, Z1), ("A2", LOW, ZXY, Z2), ("A3", LOW, ZXY, Z3),
+        ("F2", TOP, ZXY, Z2),
     ),
     (
-        ("F2", LOW, ZXY, Z3), ("A3", TOP, ZXY, Z3), ("F3", TOP, YZX, Z0), ("F2", MID, ZXY, Z0), ("A3", TOP, YZX, Z1),
-        ("A1", MID, FACTOR), ("F3", MID, ZXY, Z3), ("A1", TOP, FACTOR), ("F2", MID, YZX), ("A3", TOP, YZX, Z2),
-        ("F1", TOP, FACTOR), ("F1", LOW, YZX), ("F1", MID, FACTOR), ("F3", TOP, ZXY, Z3), ("F3", TOP, XYZ),
-        ("A3", TOP, ZXY, Z2), ("A3", TOP, ZXY, Z1), ("A3", LOW, ZXY, Z3), ("A1", LOW, FACTOR), ("A2", TOP, FACTOR),
-        ("F2", MID, ZXY, Z2), ("A2", MID, FACTOR), ("A3", MID, YZX, Z3), ("A2", LOW, YZX), ("F3", TOP, YZX, Z3),
-        ("F1", LOW, FACTOR), ("A3", TOP, ZXY, Z0), ("A2", LOW, ZXY, Z2), ("D", TOP, ZXY, Z3), ("F2", MID, FACTOR),
-        ("D", TOP, YZX, Z0), ("D", TOP, XYZ), ("F2", TOP, FACTOR), ("D", TOP, YZX, Z3), ("F3", TOP, YZX, Z2),
-        ("A3", MID, YZX, Z1), ("A3", TOP, FACTOR), ("D", MID, ZXY, Z3), ("A2", LOW, FACTOR), ("A3", MID, XYZ),
-        ("F2", LOW, ZXY, Z0), ("F3", TOP, YZX, Z1), ("F3", TOP, ZXY, Z1), ("F3", MID, YZX, Z1), ("F3", TOP, FACTOR),
-        ("F3", TOP, ZXY, Z0), ("F3", TOP, ZXY, Z2), ("F2", LOW, XYZ), ("F2", LOW, FACTOR), ("D", TOP, YZX, Z2),
-        ("A3", MID, ZXY, Z2), ("F2", LOW, ZXY, Z2), ("A3", MID, FACTOR), ("D", TOP, FACTOR), ("D", TOP, ZXY, Z1),
+        ("A1", LOW, FACTOR), ("A1", MID, FACTOR), ("A2", LOW, XYZ), ("A3", TOP, YZX, Z0), ("A3", TOP, ZXY, Z2),
+        ("F3", TOP, YZX, Z3), ("F1", LOW, FACTOR), ("F2", MID, YZX), ("A3", TOP, YZX, Z2), ("F2", MID, ZXY, Z3),
+        ("F1", MID, FACTOR), ("A1", TOP, FACTOR), ("F2", TOP, ZXY, Z0), ("A2", MID, ZXY, Z0), ("A2", MID, ZXY, Z2),
+        ("F2", MID, XYZ), ("F3", TOP, YZX, Z1), ("F3", TOP, XYZ), ("F2", LOW, ZXY, Z2), ("F1", TOP, FACTOR),
+        ("A2", MID, FACTOR), ("F3", TOP, YZX, Z2), ("F2", MID, ZXY, Z0), ("F3", TOP, ZXY, Z2), ("A2", LOW, YZX),
+        ("A3", TOP, ZXY, Z1), ("F2", MID, ZXY, Z1), ("A3", TOP, ZXY, Z0), ("A2", TOP, FACTOR), ("A3", MID, YZX, Z3),
+        ("F2", TOP, FACTOR), ("F2", MID, ZXY, Z2), ("A3", MID, ZXY, Z3), ("F2", MID, FACTOR), ("A3", MID, YZX, Z2),
+        ("A3", TOP, FACTOR), ("F3", TOP, ZXY, Z3), ("A3", MID, XYZ), ("F3", TOP, ZXY, Z1), ("A3", MID, YZX, Z0),
+        ("F3", TOP, ZXY, Z0), ("F3", TOP, FACTOR), ("A2", LOW, FACTOR), ("A3", MID, FACTOR), ("A3", MID, ZXY, Z1),
+        ("D", TOP, XYZ), ("F3", MID, YZX, Z0), ("D", TOP, YZX, Z1), ("D", TOP, YZX, Z3), ("A3", MID, ZXY, Z2),
+        ("D", TOP, ZXY, Z3), ("D", TOP, FACTOR), ("F2", LOW, YZX), ("F3", LOW, ZXY, Z3), ("F2", LOW, FACTOR),
+        ("D", TOP, ZXY, Z2), ("F3", MID, YZX, Z3),
     ),
 )
 BEFORE_STEP = {
     1: (
-        ("F2", LOW, YZX), ("A3", MID, YZX, Z2), ("D", TOP, ZXY, Z2), ("F3", MID, FACTOR), ("A3", MID, ZXY, Z1),
-        ("A3", MID, ZXY, Z0), ("D", TOP, YZX, Z1), ("A3", MID, YZX, Z0),
+        ("F2", LOW, XYZ), ("F3", MID, YZX, Z2), ("D", TOP, ZXY, Z0), ("F3", TOP, YZX, Z0), ("D", TOP, YZX, Z2),
+        ("F3", MID, FACTOR),
+    ),
+    2: (
+        ("A2", LOW, ZXY, Z1),
     ),
     4: (
-        ("F3", MID, XYZ),
+        ("F3", MID, ZXY, Z3), ("D", TOP, ZXY, Z1),
     ),
     5: (
-        ("F3", MID, YZX, Z3), ("A3", LOW, FACTOR), ("A3", LOW, XYZ), ("D", TOP, ZXY, Z0), ("F3", MID, ZXY, Z2),
+        ("D", MID, YZX, Z2), ("F3", MID, ZXY, Z2), ("F3", MID, XYZ), ("F3", MID, ZXY, Z1), ("D", MID, FACTOR),
+        ("A3", MID, ZXY, Z0), ("D", MID, YZX, Z0), ("A3", MID, YZX, Z1), ("D", MID, YZX, Z3),
     ),
     6: (
-        ("A3", LOW, ZXY, Z2), ("F3", MID, YZX, Z2), ("A3", LOW, YZX, Z3), ("D", MID, FACTOR), ("F3", MID, ZXY, Z1),
+        ("A3", LOW, ZXY, Z2), ("F2", LOW, ZXY, Z1), ("D", TOP, YZX, Z0),
+    ),
+    7: (
+        ("A3", LOW, YZX, Z3), ("A3", LOW, FACTOR), ("D", MID, ZXY, Z2),
     ),
     8: (
-        ("D", MID, YZX, Z3), ("A3", LOW, YZX, Z2), ("F3", MID, YZX, Z0), ("F3", LOW, ZXY, Z3), ("D", MID, YZX, Z2),
-        ("D", MID, ZXY, Z2), ("D", MID, YZX, Z1), ("F3", MID, ZXY, Z0), ("F2", LOW, ZXY, Z1), ("D", MID, XYZ),
+        ("A3", LOW, XYZ), ("F3", MID, YZX, Z1), ("D", MID, ZXY, Z3), ("A3", LOW, YZX, Z2), ("D", MID, XYZ),
+    ),
+    10: (
+        ("D", MID, ZXY, Z1),
     ),
     11: (
-        ("F3", LOW, YZX, Z3),
+        ("F3", MID, ZXY, Z0), ("A3", LOW, YZX, Z1), ("F3", LOW, YZX, Z3),
     ),
     12: (
-        ("F3", LOW, FACTOR), ("D", MID, ZXY, Z1),
+        ("A3", LOW, ZXY, Z1), ("D", MID, YZX, Z1),
     ),
     13: (
-        ("F3", LOW, ZXY, Z2), ("F3", LOW, YZX, Z2),
+        ("F3", LOW, FACTOR),
     ),
     14: (
-        ("F3", LOW, XYZ), ("D", MID, ZXY, Z0), ("D", MID, YZX, Z0), ("A3", LOW, YZX, Z1), ("D", LOW, ZXY, Z3),
-        ("A3", LOW, ZXY, Z1), ("A3", LOW, YZX, Z0), ("A3", LOW, ZXY, Z0),
+        ("F3", LOW, XYZ), ("D", LOW, ZXY, Z3), ("F3", LOW, YZX, Z2), ("F3", LOW, ZXY, Z2), ("D", MID, ZXY, Z0),
     ),
     15: (
-        ("D", LOW, FACTOR), ("D", LOW, ZXY, Z2), ("D", LOW, YZX, Z2),
+        ("D", LOW, FACTOR),
     ),
     16: (
+        ("F3", LOW, ZXY, Z1), ("A3", LOW, ZXY, Z0), ("D", LOW, ZXY, Z2), ("F3", LOW, YZX, Z1), ("A3", LOW, YZX, Z0),
         ("D", LOW, YZX, Z3), ("D", LOW, XYZ),
     ),
     17: (
-        ("F3", LOW, ZXY, Z1), ("F3", LOW, YZX, Z1),
+        ("D", LOW, YZX, Z2),
+    ),
+    19: (
+        ("D", LOW, ZXY, Z1), ("D", LOW, YZX, Z1),
     ),
     20: (
-        ("F3", LOW, ZXY, Z0), ("D", LOW, ZXY, Z1), ("D", LOW, YZX, Z1), ("F3", LOW, YZX, Z0),
+        ("F3", LOW, ZXY, Z0), ("F3", LOW, YZX, Z0),
     ),
     22: (
-        ("D", LOW, YZX, Z0), ("D", LOW, ZXY, Z0),
+        ("D", LOW, ZXY, Z0), ("D", LOW, YZX, Z0),
     ),
 }
 

time: 236 us -> 233 us (0.987)
  Pallas kernels: 228 us -> 225 us
    pallas_call x1, Pallas kernels: 228 us -> 225 us  [apply_panels(): pl.pallas_call(kernel, out_shape=jax.ShapeDtypeStruct((CHUNKS, COLS, LANE...]
where the time goes in v7:
time: 233 us
  Pallas kernels  225 us (97%)
  local copies, waits for them, and re-layouts  7.73 us (3%)
    pallas_call x1, Pallas kernels, apply_panels(): pl.pallas_call(kernel, out_shape=jax.ShapeDtypeStruct((CHUNKS, COLS, LANE...  225 us

profile of v7, /device:TPU:1, one launch (start us, length us, event | category | flops | bytes accessed | tf_op | source)
XLA Modules:
  0.0 232.7 jit_solution(2138071864635001339)
XLA Ops:
  0.0 1.5 copy.9
  1.5 0.0 copy-start
  1.5 1.2 copy.13
  2.7 0.2 copy-done
  2.9 2.8 %copy.6 = f32[192,32,32]{2,1,0:T(8,128)} copy(f32[192,32,32]{0,2,1:T(8,128)S(1)} %copy-done) | data formatting | bytes 1572864 | tf_op args[2]
  5.7 224.9 %apply_panels.1 = f32[24,64,128]{2,1,0:T(8,128)} custom-call(f32[32,6144]{1,0:T(8,128)} %bitcast.22, f32[3,24,32,128]{3,2,1,0:T(8,128)} %bitcast.18, f32[3,3,8,32,128]{4,3,2,1,0:T(8,128)} %bitcast.19, f32[24,256,32]{2,1,0:T(8,128)} %bitcast.17), custom_call_target="tpu_custom_call" | custom-call | tf_op jit(solution)/shard_map/apply_panels/pallas_call | solution.py:480
  230.6 2.1 copy_bitcast_fusion
Async XLA Ops:
  1.5 1.4 copy-start
